TPU v7x, 1024 devices: a whole 4x8x16 slice. The times are simulated.
1024 devices in a mesh: node: 32 (over y, x), local: 32 (over z, core).
Axes of the slice: x: 4, y: 8, z: 16, core: 2. Of those that a mesh axis runs over, the one named last changes fastest.
Arguments:
- tokens: bfloat16 [1024, 7168], P(('node', 'local')), may hold values from -6 to 6
- w_gate: bfloat16 [64, 1024, 7168], P('node', 'local'), may hold values from -0.0625 to 0.0625
- w_up: bfloat16 [64, 1024, 7168], P('node', 'local'), may hold values from -0.0625 to 0.0625
- w_down: bfloat16 [64, 1024, 7168], P('node', 'local'), may hold values from -0.1875 to 0.1875
- expert_ids: int32 [1024, 8], P(('node', 'local')), may hold values from 0 to 63, all different within a row
- gate_ints: int32 [1024, 8], P(('node', 'local')), may hold values from 1 to 8
Outputs:
- mixed: bfloat16 [1024, 7168], P(('node', 'local'))
Inputs may be any that keep to these rules, and one draw needn't show every extreme that they name: `expert_ids`: each row names 8 different experts.
All inputs are finite; a program needn't handle non-finite values.
Results may differ from a plain program's by a relative error of at most 0.025.
Values may be sent and summed in bfloat16 or wider, within the bound.
A program may use at most 32 MiB of HBM per device.

v0:
```python
import jax
import jax.numpy as jnp
from jax import lax
from jax.sharding import Mesh
from jax.sharding import PartitionSpec as P

CAP = 8
LOCAL = ("local_0", "local_1")
NODE_LOCAL = ("node", "local_0", "local_1")


def side_by_side(arrays, axis, split_dim, concat_dim, along):
    both = jnp.concatenate(arrays, axis=along)
    out, at, gathered = (
        lax.all_to_all(both, axis, split_axis=split_dim, concat_axis=concat_dim, tiled=True),
        0,
        [],
    )
    for a in arrays:
        gathered.append(lax.slice_in_dim(out, at, at + a.shape[along], axis=along))
        at += a.shape[along]
    return tuple(gathered)


def reduced_to_own(tiles, axes, order):
    shape = [lax.axis_size(a) for a in axes]
    tiles = tiles.reshape(*shape, *tiles.shape[1:])
    tiles = tiles.transpose(*order, *range(len(axes), tiles.ndim))
    tiles = tiles.reshape(-1, *tiles.shape[len(axes) :])
    for k in order:
        tiles = lax.psum_scatter(tiles, axes[k], scatter_dimension=0, tiled=True)
    return tiles[0]


def in_blocks(shard, dim, length):
    before, after = (shard.shape[:dim], shard.shape[dim + 1 :])
    return jnp.moveaxis(shard.reshape(*before, length, -1, *after), dim, 0)


def summed_rows(shard, axes, order, dim):
    length = lax.axis_size(axes)
    return reduced_to_own(in_blocks(shard, dim, length), axes, order)


def on_device(tokens, w_gate, w_up, w_down, expert_ids, gate_ints):
    node_count = lax.axis_size("node")
    tok_dev = tokens.shape[0]
    model_width = tokens.shape[1]
    exp_node = w_gate.shape[0]
    slot_count = node_count * tok_dev
    wanted = jnp.arange(node_count * exp_node, dtype=jnp.int32).reshape(node_count, exp_node)
    matched = expert_ids[None, :, :, None] == wanted[:, None, None, :]
    gate_sums = jnp.sum(jnp.where(matched, gate_ints[None, :, :, None], 0), axis=2)
    is_hit = jnp.sum(gate_sums, axis=-1) > 0
    outgoing = jnp.where(is_hit[:, :, None], tokens[None, :, :], jnp.zeros_like(tokens)[None, :, :])
    rows_in, gates_in = side_by_side((outgoing, gate_sums.astype(jnp.bfloat16)), "node", 0, 0, 2)
    flat_rows = rows_in.reshape(slot_count, model_width)
    flat_gates = gates_in.reshape(slot_count, exp_node)
    present = (jnp.sum(flat_gates.astype(jnp.float32), axis=-1) > 0).astype(jnp.int32)
    slot_rank = jnp.cumsum(present) - present
    picker = (
        (present[None, :] > 0) & (slot_rank[None, :] == jnp.arange(CAP, dtype=jnp.int32)[:, None])
    ).astype(jnp.bfloat16)
    packed = jnp.dot(picker, flat_rows, preferred_element_type=jnp.float32).astype(jnp.bfloat16)
    packed_gates = jnp.dot(picker, flat_gates, preferred_element_type=jnp.float32).astype(
        jnp.bfloat16
    )
    all_rows, all_gates = (
        lax.all_gather(packed, LOCAL, axis=0, tiled=True),
        lax.all_gather(packed_gates, LOCAL, axis=0, tiled=True),
    )
    gate_act = jnp.einsum("rd,efd->ref", all_rows, w_gate, preferred_element_type=jnp.float32)
    up_act = jnp.einsum("rd,efd->ref", all_rows, w_up, preferred_element_type=jnp.float32)
    scales = all_gates.astype(jnp.float32) / 8.0
    hidden = (jax.nn.silu(gate_act) * up_act * scales[:, :, None]).astype(jnp.bfloat16)
    hidden = hidden.reshape(hidden.shape[0], -1)
    down_flat = w_down.reshape(-1, model_width)
    partial_value = jnp.dot(hidden, down_flat, preferred_element_type=jnp.float32)
    summed = summed_rows(partial_value.astype(jnp.bfloat16), LOCAL, (1, 0), 0).astype(jnp.float32)
    group_out = summed.astype(jnp.bfloat16)
    unpacked = jnp.dot(picker.T, group_out, preferred_element_type=jnp.float32).astype(jnp.bfloat16)
    unpacked = unpacked.reshape(node_count, tok_dev, model_width)
    returned = lax.all_to_all(unpacked, "node", split_axis=0, concat_axis=0, tiled=True)
    return jnp.sum(returned.astype(jnp.float32), axis=0).astype(jnp.bfloat16)


def solution(mesh):
    finer = Mesh(mesh.devices.reshape(mesh.shape["node"], 16, 2), ("node", "local_0", "local_1"))
    return jax.shard_map(
        on_device,
        mesh=finer,
        in_specs=(
            P(NODE_LOCAL, None),
            P("node", LOCAL, None),
            P("node", LOCAL, None),
            P("node", LOCAL, None),
            P(NODE_LOCAL, None),
            P(NODE_LOCAL, None),
        ),
        out_specs=P(NODE_LOCAL, None),
        check_vma=False,
    )
```

profile of v0, /device:TPU:8, one launch (start us, length us, event | category | flops | bytes accessed | tf_op | source)
XLA Modules:
  0.0 276.1 jit_solution(13054360929277926606)
XLA Ops:
  6.5 0.0 copy-start
  6.5 0.0 all-gather.3.cloned.1.call-start
  6.5 0.8 select_reduce_fusion.1
  7.4 0.1 copy.33
  7.5 0.8 reduce.5
  8.3 0.7 broadcast_select_fusion
  9.0 1.0 pad_maximum_fusion
  10.0 0.5 broadcast.157
  10.5 3.5 %reduce.7 = bf16[32,7170]{1,0:T(8,128)(2,1)S(1)} reduce(bf16[32,1,7170]{2,1,0:T(2,128)(2,1)S(1)} %pad_maximum_fusion, bf16[]{:T(256)} %broadcast.157), dimensions={1}, to_apply=%pad_maximum_fusion.reduce_sub_computation | reduce | bytes 917762 | tf_op jit(solution)/shard_map/concatenate | solution.py:13
  14.1 0.5 reshape.181
  14.6 28.5 %all_to_all.10 = bf16[32,2,3585]{2,1,0:T(2,128)(2,1)S(1)} all-to-all(bf16[32,2,3585]{2,1,0:T(2,128)(2,1)S(1)} %reshape.181), channel_id=1, replica_groups=mesh['node'=32,'local_0'=16,'local_1'=2] {'node'}, dimensions={0} | all-to-all | bytes 917760 | tf_op jit(solution)/shard_map/all_to_all | solution.py:15
  43.1 0.8 reshape.182
  43.9 0.9 slice.9
  44.8 0.0 copy-start.1
  44.8 0.1 copy.34
  45.0 0.1 copy.35
  45.0 0.1 reduce-window.8
  45.1 0.1 reduce.6
  45.2 0.9 convolution_convert_fusion.1
  46.1 0.0 all-gather.3.cloned.1.call-update
  46.1 0.0 reduce-scatter.3.cloned.1.call-start
  46.2 0.1 fusion.17
  46.3 41.0 %all-gather = bf16[32,8,2]{1,2,0:T(2,128)(2,1)S(1)} all-gather(bf16[1,8,2]{1,2,0:T(2,128)(2,1)S(1)} %fusion.17), channel_id=1, replica_groups=mesh['node'=32,'local_0'=16,'local_1'=2] {'local_0','local_1'}, dimensions={0}, use_global_device_ids=true | all-gather | bytes 1056 | tf_op jit(solution)/shard_map/all_gather | solution.py:70
  87.3 0.1 copy.37
  87.4 0.1 copy.38
  87.5 0.1 reshape.176
  87.6 35.8 %all-gather.3.cloned.1.call-done = bf16[256,7168]{1,0:T(8,128)(2,1)} async-done(((bf16[8,7168]{1,0:T(8,128)(2,1)}), bf16[256,7168]{1,0:T(8,128)(2,1)}) %all-gather.3.cloned.1.call-update) | async-done | bytes 3670032 | tf_op jit(solution)/shard_map/all_gather | solution.py:69
  123.4 3.5 %fusion.4 = f32[256,2,32]{0,2,1:T(8,128)S(1)} fusion(bf16[2,32,7168]{2,1,0:T(8,128)(2,1)} %param.7, bf16[256,7168]{1,0:T(8,128)(2,1)} %all-gather.3.cloned.1.call-done), kind=kOutput, calls=%fused_computation.7 | convolution fusion | flops 234881024 | bytes 4653056 | tf_op jit(solution)/shard_map/rd,efd->ref/dot_general | solution.py:72
  126.9 0.0 copy-done
  126.9 0.0 copy-done.1
  126.9 8.0 %fusion = bf16[256,7168]{1,0:T(8,128)(2,1)} fusion(bf16[2,32,7168]{2,1,0:T(8,128)(2,1)S(1)} %copy-done, bf16[2,32,7168]{2,1,0:T(8,128)(2,1)S(1)} %copy-done.1, bf16[256,7168]{1,0:T(8,128)(2,1)} %all-gather.3.cloned.1.call-done, f32[256,2,32]{0,2,1:T(8,128)S(1)} %fusion.4, f32[256,2]{0,1:T(2,128)S(1)} %reshape.176), kind=kOutput, calls=%fused_computation.1 | convolution fusion | flops 471711744 | bytes 9242624 | tf_op jit(solution)/shard_map/dot_general | solution.py:78
  134.9 4.1 %copy.39 = bf16[16,2,8,7168]{3,2,0,1:T(8,128)(2,1)} copy(bf16[16,2,8,7168]{3,2,1,0:T(8,128)(2,1)} %bitcast.47) | data formatting | bytes 7340032 | tf_op jit(solution)/shard_map/reshape;reshape | solution.py:27
  139.0 0.0 reduce-scatter.3.cloned.1.call-update
  139.0 0.0 reduce-scatter.5.cloned.1.call-start
  139.0 21.7 %reduce-scatter.3.cloned.1.call-done = bf16[16,8,7168]{2,1,0:T(8,128)(2,1)} async-done(((bf16[32,8,7168]{2,1,0:T(8,128)(2,1)}), bf16[16,8,7168]{2,1,0:T(8,128)(2,1)}) %reduce-scatter.3.cloned.1.call-update) | async-done | bytes 1835024 | tf_op jit(solution)/shard_map/reduce_scatter | solution.py:31
  160.8 0.0 reduce-scatter.5.cloned.1.call-update
  160.8 82.2 %reduce-scatter.5.cloned.1.call-done = bf16[1,8,7168]{2,1,0:T(8,128)(2,1)} async-done(((bf16[16,8,7168]{2,1,0:T(8,128)(2,1)}), bf16[1,8,7168]{2,1,0:T(8,128)(2,1)}) %reduce-scatter.5.cloned.1.call-update) | async-done | bytes 114704 | tf_op jit(solution)/shard_map/reduce_scatter | solution.py:31
  243.0 1.2 fusion.1
  244.2 0.9 reduce.8
  245.2 0.3 reshape.183
  245.5 22.2 %all_to_all.11 = bf16[32,2,3584]{2,1,0:T(2,128)(2,1)S(1)} all-to-all(bf16[32,2,3584]{2,1,0:T(2,128)(2,1)S(1)} %reshape.183), channel_id=1, replica_groups=mesh['node'=32,'local_0'=16,'local_1'=2] {'node'}, dimensions={0} | all-to-all | bytes 917504 | tf_op jit(solution)/shard_map/all_to_all | solution.py:83
  267.7 0.4 reshape.184
  268.1 0.8 reduce_sum.44
  268.9 0.6 reduce_sum.45
  (8 shorter events, 0.1 us)
Async XLA Ops:
  6.5 120.3 %copy-start = (bf16[2,32,7168]{2,1,0:T(8,128)(2,1)S(1)}, bf16[2,32,7168]{2,1,0:T(8,128)(2,1)}, u32[]{:S(2)}) copy-start(bf16[2,32,7168]{2,1,0:T(8,128)(2,1)} %param.9) | copy-start | bytes 2752516
  6.5 116.8 %all-gather.3.cloned.1.call-start = ((), (), s32[]{:S(2)}) async-start(), calls=%async_computation.4 | async-start | bytes 3784704 | tf_op jit(solution)/shard_map/all_gather | solution.py:69
  44.8 82.1 %copy-start.1 = (bf16[2,32,7168]{2,1,0:T(8,128)(2,1)S(1)}, bf16[2,32,7168]{2,1,0:T(8,128)(2,1)}, u32[]{:S(2)}) copy-start(bf16[2,32,7168]{2,1,0:T(8,128)(2,1)} %param.8) | copy-start | bytes 2752516
  46.1 114.6 %reduce-scatter.3.cloned.1.call-start = ((), (), s32[]{:S(2)}) async-start(), calls=%async_computation.5 | async-start | bytes 5505024 | tf_op jit(solution)/shard_map/reduce_scatter | solution.py:31
  139.0 104.0 %reduce-scatter.5.cloned.1.call-start = ((), (), s32[]{:S(2)}) async-start(), calls=%async_computation.6 | async-start | bytes 1949696 | tf_op jit(solution)/shard_map/reduce_scatter | solution.py:31
Sparse Core Ops, SparseCore 0:
  46.3 77.0 all-gather.2
  139.1 21.6 reduce-scatter.2
  164.2 78.7 reduce-scatter.4
where the time goes:
time: 276 us
  waiting for transfers between devices  140 us (51%)
  blocking collectives  91.7 us (33%)
  matrix products  13.7 us (5%)
  between operations  13.2 us (5%)
  other arithmetic  8.83 us (3%)
  local copies, waits for them, and re-layouts  8.74 us (3%)
    reduce_scatter x2, waiting for transfers between devices, reduced_to_own(): tiles = lax.psum_scatter(tiles, axes[k], scatter_dimension=0, tiled=True)  104 us
    all_gather x1, blocking collectives, on_device(): lax.all_gather(packed_gates, LOCAL, axis=0, tiled=True)  41 us
    all_gather x1, waiting for transfers between devices, on_device(): lax.all_gather(packed, LOCAL, axis=0, tiled=True)  35.8 us
    all_to_all x1, blocking collectives, side_by_side(): lax.all_to_all(both, axis, split_axis=split_dim, concat_axis=concat_dim,...  28.5 us
    all_to_all x1, blocking collectives, on_device(): lax.all_to_all(unpacked, 'node', split_axis=0, concat_axis=0, tiled=True)  22.2 us
    dot_general x1, matrix products, on_device(): jnp.dot(hidden, down_flat, preferred_element_type=jnp.float32)  7.97 us
  transfers between devices with their start and end apart: 3, of which 3 were waited for; matrix products, arithmetic and copies ran while one was open for 0% of the time, Pallas kernels for 0%

commit v1 on v0

v1 whole, which is shorter than its diff:
```python
import functools

import jax
import jax.numpy as jnp
from jax import lax
from jax.experimental import pallas as pl
from jax.experimental.pallas import tpu as pltpu
from jax.sharding import PartitionSpec as P

CAP = 8
NX = 4
CHUNKS = 4
META = 128
BF16 = jnp.bfloat16
F32 = jnp.float32
MESH_ID = pl.DeviceIdType.MESH


def layer_kernel(
    nx, ny, nz,
    tok_ref, wg_ref, wu_ref, wd_ref, ids_ref, gates_ref,
    out_ref,
    t1, t2, xbuf, wgu, wdn, zbuf, hbuf, pbuf, rsend, rrecv, ysend, yrecv, fsend, frecv,
    wl_sem, ws_sem, wr_sem, s1, r1, s2, r2, sa, ra, ss, rs, s3, r3, s4, r4,
):
    half = wgu.shape[-1]
    width = half // CHUNKS
    offs = [0] + [META + q * width for q in range(1, CHUNKS)]
    lens = [META + width] + [width] * (CHUNKS - 1)
    d_off = [META + q * width for q in range(CHUNKS)]
    hz = nz // 2
    n = lax.axis_index("node")
    l = lax.axis_index("local")
    x, y = lax.rem(n, nx), n // nx
    z, c = l // 2, lax.rem(l, 2)

    def at_x(v):
        return (y * nx + v, l)

    def at_y(v):
        return (v * nx + x, l)

    def at_z(v):
        return (n, v * 2 + c)

    up, down = lax.rem(z + 1, nz), lax.rem(z + nz - 1, nz)
    partner = (n, z * 2 + 1 - c)
    xs = [lax.rem(x + d, nx) for d in range(1, nx)]
    ys = [lax.rem(y + d, ny) for d in range(1, ny)]

    def push(src, dst, send, recv, device):
        pltpu.make_async_remote_copy(
            src_ref=src, dst_ref=dst, send_sem=send, recv_sem=recv,
            device_id=device, device_id_type=MESH_ID,
        ).start()

    def await_bytes(ref, sem):
        pltpu.make_async_copy(ref, ref, sem).wait()

    local = []
    for h in range(2):
        cols = pl.ds(h * half, half)
        local.append(pltpu.make_async_copy(wg_ref.at[:, :, cols], wgu.at[h, 0, 0], wl_sem.at[0, h]))
        local.append(pltpu.make_async_copy(wu_ref.at[:, :, cols], wgu.at[h, 1, 0], wl_sem.at[1, h]))
        local.append(pltpu.make_async_copy(wd_ref.at[:, :, cols], wdn.at[h, 0], wl_sem.at[2, h]))
    for copy in local:
        copy.start()

    barrier = pltpu.get_barrier_semaphore()
    greeted = [partner, at_z(up), at_z(down)] + [at_x(v) for v in xs] + [at_y(v) for v in ys]
    for device in greeted:
        pl.semaphore_signal(barrier, 1, device_id=device, device_id_type=MESH_ID)

    lane = lax.broadcasted_iota(jnp.int32, (2, META), 1)
    row = lax.broadcasted_iota(jnp.int32, (2, META), 0)
    gates = jnp.zeros((2, META), jnp.int32)
    for k in range(ids_ref.shape[1]):
        gates += jnp.where((lane == ids_ref[0, k]) & (row == 0), gates_ref[0, k], 0)
    t1[y, :, 0:META] = gates.astype(F32).astype(BF16)
    tok = tok_ref[...].astype(F32)
    pair = jnp.concatenate([tok[:, :half], tok[:, half:]], axis=0)
    t1[y, :, META:] = pair.astype(BF16)

    pl.semaphore_wait(barrier, len(greeted))

    def part(q):
        return pl.ds(offs[q], lens[q])

    for q in range(CHUNKS):
        for v in ys:
            own = t1.at[y, :, part(q)]
            push(own, own, s1.at[q], r1.at[q], at_y(v))
    for h in range(2):
        cols = pl.ds(h * half, half)
        push(wg_ref.at[:, :, cols], wgu.at[h, 0, 1], ws_sem.at[0, h], wr_sem.at[0, h], partner)
        push(wu_ref.at[:, :, cols], wgu.at[h, 1, 1], ws_sem.at[1, h], wr_sem.at[1, h], partner)
        push(wd_ref.at[:, :, cols], wdn.at[h, 1], ws_sem.at[2, h], wr_sem.at[2, h], partner)

    for q in range(CHUNKS):
        await_bytes(t1.at[pl.ds(0, ny - 1), :, part(q)], r1.at[q])
        for v in range(ny):
            t2[x, 2 * v : 2 * v + 2, part(q)] = t1[v, :, part(q)]
        for v in xs:
            own = t2.at[x, :, part(q)]
            push(own, own, s2.at[q], r2.at[q], at_x(v))

    cells = nx * ny * 2
    rows = CAP * 2

    def order(i):
        return ((i // 2) % ny) * nx + i // (2 * ny)

    i0 = lax.broadcasted_iota(jnp.int32, (cells, cells), 0)
    i1 = lax.broadcasted_iota(jnp.int32, (cells, cells), 1)
    same = (i0 // 2 == i1 // 2).astype(F32).astype(BF16)
    before = (order(i0) < order(i1)).astype(F32).astype(BF16)
    after = (order(i1) < order(i0)).astype(F32).astype(BF16)
    mine = lax.broadcasted_iota(jnp.int32, (rows, META), 1)
    mine = ((mine // 2) == n).astype(F32).astype(BF16)

    picker = None
    picker_t = None
    for q in range(CHUNKS):
        await_bytes(t2.at[pl.ds(0, nx - 1), :, part(q)], r2.at[q])
        if q == 0:
            meta = t2[:, :, 0:META].reshape(cells, META)
            nt = (((1,), (1,)), ((), ()))
            total = lax.dot_general(mine, meta, nt, preferred_element_type=F32)
            hit = (total > 0).astype(F32).astype(BF16)
            rank = jnp.dot(hit, before, preferred_element_type=F32)
            hit = jnp.dot(hit, same, preferred_element_type=F32)
            r = lax.broadcasted_iota(jnp.int32, (rows, cells), 0)
            i = lax.broadcasted_iota(jnp.int32, (rows, cells), 1)
            picks = (hit > 0) & (rank == (r // 2).astype(F32)) & (r % 2 == i % 2)
            picker = picks.astype(F32).astype(BF16)
            total = lax.dot_general(meta, mine, nt, preferred_element_type=F32)
            hit = (total > 0).astype(F32).astype(BF16)
            rank = jnp.dot(after, hit, preferred_element_type=F32)
            hit = jnp.dot(same, hit, preferred_element_type=F32)
            r = lax.broadcasted_iota(jnp.int32, (cells, rows), 1)
            i = lax.broadcasted_iota(jnp.int32, (cells, rows), 0)
            picks = (hit > 0) & (rank == (r // 2).astype(F32)) & (r % 2 == i % 2)
            picker_t = picks.astype(F32).astype(BF16)
        field = t2[:, :, part(q)].reshape(cells, lens[q])
        xbuf[z, :, part(q)] = jnp.dot(picker, field, preferred_element_type=F32).astype(BF16)
        own = xbuf.at[z, :, part(q)]
        push(own, own, sa.at[q], ra.at[0, 1, q], at_z(up))
        push(own, own, sa.at[q], ra.at[1, 1, q], at_z(down))

    def hop(s, carry):
        below = lax.rem(z + nz - s, nz)
        above = lax.rem(z + s, nz)
        for q in range(CHUNKS):
            block = xbuf.at[below, :, part(q)]
            await_bytes(block, ra.at[0, s, q])
            push(block, block, sa.at[q], ra.at[0, s + 1, q], at_z(up))
            block = xbuf.at[above, :, part(q)]
            await_bytes(block, ra.at[1, s, q])
            @pl.when(s < hz - 1)
            def _():
                push(block, block, sa.at[q], ra.at[1, s + 1, q], at_z(down))
        return carry

    lax.fori_loop(1, hz, hop, 0)
    for q in range(CHUNKS):
        await_bytes(xbuf.at[lax.rem(z + hz, nz), :, part(q)], ra.at[0, hz, q])

    for copy in local:
        copy.wait()
    for h in range(2):
        await_bytes(wgu.at[h, 0, 1], wr_sem.at[0, h])
        await_bytes(wgu.at[h, 1, 1], wr_sem.at[1, h])
        await_bytes(wdn.at[h, 1], wr_sem.at[2, h])
    pair_rows = nz * rows
    tokens = pair_rows // 2
    units = wdn.shape[1] * wdn.shape[2] * wdn.shape[3]
    for q in range(CHUNKS):
        piece = xbuf[:, :, pl.ds(d_off[q], width)].reshape(pair_rows, width)
        for h in range(2):
            w = wgu[h, :, :, :, :, pl.ds(q * width, width)].reshape(2 * units, width)
            nt = (((1,), (1,)), ((), ()))
            v = lax.dot_general(piece, w, nt, preferred_element_type=F32)
            for k in range(2):
                if q == 0:
                    zbuf[h, k] = v[:, k * units : (k + 1) * units]
                else:
                    zbuf[h, k] += v[:, k * units : (k + 1) * units]
    lane = lax.broadcasted_iota(jnp.int32, (META, units), 0)
    unit = lax.broadcasted_iota(jnp.int32, (META, units), 1)
    ffl = wdn.shape[3]
    chosen = (lane == 2 * n + (unit // ffl) % 2).astype(F32).astype(BF16)
    gate_rows = xbuf[:, :, 0:META].reshape(pair_rows, META)
    hbuf[0] = jnp.dot(gate_rows, chosen, preferred_element_type=F32)
    even, odd = pl.ds(0, tokens, 2), pl.ds(1, tokens, 2)
    gate_act = zbuf[0, 0, even, :] + zbuf[1, 0, odd, :]
    up_act = zbuf[0, 1, even, :] + zbuf[1, 1, odd, :]
    scale = hbuf[0, even, :] / 8.0
    hidden = gate_act / (1.0 + jnp.exp(-gate_act)) * up_act * scale
    none = jnp.zeros_like(hidden)
    hbuf[0, even, :] = hidden
    hbuf[1, even, :] = none
    hbuf[0, odd, :] = none
    hbuf[1, odd, :] = hidden
    hidden = jnp.concatenate([hbuf[0], hbuf[1]], axis=1).astype(BF16)
    for q in range(CHUNKS):
        w = wdn[:, :, :, :, pl.ds(q * width, width)].reshape(2 * units, width)
        v = jnp.dot(hidden, w, preferred_element_type=F32)
        pbuf[:, :, pl.ds(q * width, width)] = v.reshape(nz, rows, width)

    def slot(direction, step):
        return direction * hz + step - 1

    def cols(q):
        return pl.ds(q * width, width)

    for q in range(CHUNKS):
        far = lax.rem(z + hz, nz)
        rsend[slot(0, 1), :, cols(q)] = pbuf[far, :, cols(q)].astype(BF16)
        push(rsend.at[slot(0, 1), :, cols(q)], rrecv.at[slot(0, 1), :, cols(q)], ss.at[q], rs.at[0, 1, q], at_z(up))
        far = lax.rem(z + hz + 1, nz)
        rsend[slot(1, 1), :, cols(q)] = pbuf[far, :, cols(q)].astype(BF16)
        push(rsend.at[slot(1, 1), :, cols(q)], rrecv.at[slot(1, 1), :, cols(q)], ss.at[q], rs.at[1, 1, q], at_z(down))

    def back(s, carry):
        above = lax.rem(z + hz + 1 - s, nz)
        below = lax.rem(z + hz + s, nz)
        for q in range(CHUNKS):
            got = rrecv.at[slot(0, s - 1), :, cols(q)]
            await_bytes(got, rs.at[0, s - 1, q])
            rsend[slot(0, s), :, cols(q)] = (got[...].astype(F32) + pbuf[above, :, cols(q)]).astype(BF16)
            push(rsend.at[slot(0, s), :, cols(q)], rrecv.at[slot(0, s), :, cols(q)], ss.at[q], rs.at[0, s, q], at_z(up))
            @pl.when(s < hz)
            def _():
                got = rrecv.at[slot(1, s - 1), :, cols(q)]
                await_bytes(got, rs.at[1, s - 1, q])
                rsend[slot(1, s), :, cols(q)] = (got[...].astype(F32) + pbuf[below, :, cols(q)]).astype(BF16)
                push(rsend.at[slot(1, s), :, cols(q)], rrecv.at[slot(1, s), :, cols(q)], ss.at[q], rs.at[1, s, q], at_z(down))
        return carry

    lax.fori_loop(2, hz + 1, back, 0)

    for q in range(CHUNKS):
        await_bytes(rrecv.at[slot(1, hz - 1), :, cols(q)], rs.at[1, hz - 1, q])
        await_bytes(rrecv.at[slot(0, hz), :, cols(q)], rs.at[0, hz, q])
        total = pbuf[z, :, cols(q)] + rrecv[slot(0, hz), :, cols(q)].astype(F32) + rrecv[slot(1, hz - 1), :, cols(q)].astype(F32)
        placed = jnp.dot(picker_t, total.astype(BF16), preferred_element_type=F32)
        ysend[:, :, cols(q)] = placed.astype(BF16).reshape(nx, 2 * ny, width)
        for v in xs:
            push(ysend.at[v, :, cols(q)], yrecv.at[x, :, cols(q)], s3.at[q], r3.at[q], at_x(v))
    for q in range(CHUNKS):
        await_bytes(yrecv.at[pl.ds(0, nx - 1), :, cols(q)], r3.at[q])
        total = ysend[x, :, cols(q)].astype(F32)
        for v in xs:
            total += yrecv[v, :, cols(q)].astype(F32)
        total = total.astype(BF16)
        for v in range(ny):
            fsend[v, :, cols(q)] = total[2 * v : 2 * v + 2, :]
        for v in ys:
            push(fsend.at[v, :, cols(q)], frecv.at[y, :, cols(q)], s4.at[q], r4.at[q], at_y(v))
    for q in range(CHUNKS):
        await_bytes(frecv.at[pl.ds(0, ny - 1), :, cols(q)], r4.at[q])
        total = fsend[y, :, cols(q)].astype(F32)
        for v in ys:
            total += frecv[v, :, cols(q)].astype(F32)
        total = total.astype(BF16)
        out_ref[0:1, pl.ds(q * width, width)] = total[0:1, :]
        out_ref[0:1, pl.ds(half + q * width, width)] = total[1:2, :]

    for q in range(CHUNKS):
        await_bytes(t1.at[pl.ds(0, ny - 1), :, part(q)], s1.at[q])
        await_bytes(t2.at[pl.ds(0, nx - 1), :, part(q)], s2.at[q])
        await_bytes(xbuf.at[pl.ds(0, nz - 1), :, part(q)], sa.at[q])
        await_bytes(rrecv.at[pl.ds(0, nz - 1), :, cols(q)], ss.at[q])
        await_bytes(yrecv.at[pl.ds(0, nx - 1), :, cols(q)], s3.at[q])
        await_bytes(frecv.at[pl.ds(0, ny - 1), :, cols(q)], s4.at[q])
    for h in range(2):
        await_bytes(wgu.at[h, 0, 1], ws_sem.at[0, h])
        await_bytes(wgu.at[h, 1, 1], ws_sem.at[1, h])
        await_bytes(wdn.at[h, 1], ws_sem.at[2, h])


def solution(mesh):
    nodes, locals_ = mesh.shape["node"], mesh.shape["local"]
    nx = min(NX, nodes)
    ny, nz = nodes // nx, locals_ // 2
    hz = nz // 2

    def on_device(tokens, w_gate, w_up, w_down, expert_ids, gate_ints):
        model_width = tokens.shape[1]
        half = model_width // 2
        exp_node, ffl = w_gate.shape[0], w_gate.shape[1]
        units = 2 * exp_node * ffl
        rows = 2 * CAP
        sem = pltpu.SemaphoreType.DMA
        any_space = pl.BlockSpec(memory_space=pl.ANY)
        vmem = pl.BlockSpec(memory_space=pltpu.VMEM)
        smem = pl.BlockSpec(memory_space=pltpu.SMEM)
        return pl.pallas_call(
            functools.partial(layer_kernel, nx, ny, nz),
            out_shape=jax.ShapeDtypeStruct((1, model_width), BF16),
            in_specs=[vmem, any_space, any_space, any_space, smem, smem],
            out_specs=vmem,
            scratch_shapes=[
                pltpu.VMEM((ny, 2, META + half), BF16),
                pltpu.VMEM((nx, 2 * ny, META + half), BF16),
                pltpu.VMEM((nz, rows, META + half), BF16),
                pltpu.VMEM((2, 2, 2, exp_node, ffl, half), BF16),
                pltpu.VMEM((2, 2, exp_node, ffl, half), BF16),
                pltpu.VMEM((2, 2, nz * rows, units), F32),
                pltpu.VMEM((2, nz * rows, units), F32),
                pltpu.VMEM((nz, rows, half), F32),
                pltpu.VMEM((nz, rows, half), BF16),
                pltpu.VMEM((nz, rows, half), BF16),
                pltpu.VMEM((nx, 2 * ny, half), BF16),
                pltpu.VMEM((nx, 2 * ny, half), BF16),
                pltpu.VMEM((ny, 2, half), BF16),
                pltpu.VMEM((ny, 2, half), BF16),
                sem((3, 2)), sem((3, 2)), sem((3, 2)),
                sem((CHUNKS,)), sem((CHUNKS,)), sem((CHUNKS,)), sem((CHUNKS,)),
                sem((CHUNKS,)), sem((2, hz + 1, CHUNKS)),
                sem((CHUNKS,)), sem((2, hz + 1, CHUNKS)),
                sem((CHUNKS,)), sem((CHUNKS,)), sem((CHUNKS,)), sem((CHUNKS,)),
            ],
            compiler_params=pltpu.CompilerParams(
                collective_id=0, has_side_effects=True, vmem_limit_bytes=60 * 1024 * 1024
            ),
            name="layer",
        )(tokens, w_gate, w_up, w_down, expert_ids, gate_ints)

    both = P(("node", "local"), None)
    weights = P("node", "local", None)
    return jax.shard_map(
        on_device, mesh=mesh,
        in_specs=(both, weights, weights, weights, both, both),
        out_specs=both, check_vma=False,
    )
```

time: 276 us -> 102 us (0.37)
  the two profiles are of different devices: /device:TPU:8 before, /device:TPU:4 now
where the time goes in v1:
time: 102 us
  Pallas kernels  101 us (99%)
  local copies, waits for them, and re-layouts  1.39 us (1%)
    pallas_call x1, Pallas kernels, on_device(): pl.pallas_call(functools.partial(layer_kernel, nx, ny, nz), out_shape=jax...  101 us

profile of v1, /device:TPU:4, one launch (start us, length us, event | category | flops | bytes accessed | tf_op | source)
XLA Modules:
  0.0 102.0 jit_solution(11186684642023922097)
XLA Ops:
  0.0 100.6 %layer.1 = bf16[1,7168]{1,0:T(2,128)(2,1)} custom-call(bf16[1,7168]{1,0:T(2,128)(2,1)} %tok_ref.1, bf16[2,32,7168]{2,1,0:T(8,128)(2,1)} %wg_ref.1, bf16[2,32,7168]{2,1,0:T(8,128)(2,1)} %wu_ref.1, bf16[2,32,7168]{2,1,0:T(8,128)(2,1)} %wd_ref.1, s32[1,8]{1,0:T(1,128)} %ids_ref.1, s32[1,8]{1,0:T(1,128)} %gates_ref.1), custom_call_target="tpu_custom_call" | custom-call | tf_op jit(solution)/shard_map/layer/pallas_call | solution.py:298
  100.6 1.4 %copy.8 = bf16[1,7168]{1,0:T(2,128)(2,1)} copy(bf16[1,7168]{1,0:T(2,128)(2,1)} %layer.1) | data formatting | bytes 28672

commit v2 on v0

v2 whole, which is shorter than its diff:
```python
import functools

import jax
import jax.numpy as jnp
from jax import lax
from jax.experimental import pallas as pl
from jax.experimental.pallas import tpu as pltpu
from jax.sharding import PartitionSpec as P

CAP = 8
NX = 4
CHUNKS = 7
META = 128
BF16 = jnp.bfloat16
F32 = jnp.float32
MESH_ID = pl.DeviceIdType.MESH
NT = (((1,), (1,)), ((), ()))
scope = jax.named_scope


def ones(mask):
    return mask.astype(F32).astype(BF16)


def layer_kernel(
    nx, ny, nz,
    tok_ref, wg_ref, wu_ref, wd_ref, ids_ref, gates_ref,
    out_ref,
    tokv, idsv, gatesv, tsend, t1, t2, xbuf, wgu, wdn, zbuf, hbuf, pfar, pnear, rsend, rrecv,
    ysend, yrecv, fsend, frecv,
    in_sem, wl_sem, ws_sem, wr_sem, s0, s1, r1, s2, r2, sa, ra, sx, rx, sp, rp, ss, rs, s3, r3, s4, r4,
):
    half = wgu.shape[-1]
    width = half // CHUNKS
    offs = [0] + [META + q * width for q in range(1, CHUNKS)]
    lens = [META + width] + [width] * (CHUNKS - 1)
    d_off = [META + q * width for q in range(CHUNKS)]
    hz = nz // 2
    rows = CAP * 2
    ffl = wdn.shape[3]
    units = wdn.shape[1] * wdn.shape[2] * ffl
    n = lax.axis_index("node")
    l = lax.axis_index("local")
    x, y = lax.rem(n, nx), n // nx
    z, c = l // 2, lax.rem(l, 2)
    lead = c == 1

    def at_x(v):
        return (y * nx + v, z * 2 + 1)

    def at_y(v, core):
        return (v * nx + x, z * 2 + core)

    up = (n, lax.rem(z + 1, nz) * 2 + 1)
    down = (n, lax.rem(z + nz - 1, nz) * 2 + 1)
    partner = (n, z * 2 + 1 - c)
    xs = [lax.rem(x + d, nx) for d in range(1, nx)]
    ys = [lax.rem(y + d, ny) for d in range(1, ny)]

    near = 1 + 2 * (hz - 2)
    far = 3

    def going_up(s):
        return s if s <= hz - 2 else near + s - (hz - 1)

    def going_down(s):
        return hz - 2 + s if s <= hz - 2 else near + 2

    def push(src, dst, send, recv, device):
        pltpu.make_async_remote_copy(
            src_ref=src, dst_ref=dst, send_sem=send, recv_sem=recv,
            device_id=device, device_id_type=MESH_ID,
        ).start()

    def await_bytes(ref, sem):
        pltpu.make_async_copy(ref, ref, sem).wait()

    def signal(sem, device):
        pl.semaphore_signal(sem, 1, device_id=device, device_id_type=MESH_ID)

    def part(q):
        return pl.ds(offs[q], lens[q])

    def cols(q):
        return pl.ds(q * width, width)

    barrier = pltpu.get_barrier_semaphore()
    with scope("entry"):
        signal(barrier, partner)
        for v in ys:
            signal(barrier, at_y(v, 1))

        @pl.when(lead)
        def _():
            for v in ys:
                signal(barrier, at_y(v, 0))
            for v in xs:
                signal(barrier, at_x(v))
            signal(barrier, up)
            signal(barrier, down)

        inputs = [
            pltpu.make_async_copy(tok_ref, tokv, in_sem.at[0]),
            pltpu.make_async_copy(ids_ref, idsv, in_sem.at[1]),
            pltpu.make_async_copy(gates_ref, gatesv, in_sem.at[2]),
        ]
        for copy in inputs:
            copy.start()
        for h in range(2):
            wcols = pl.ds(h * half, half)
            pltpu.make_async_copy(wg_ref.at[:, :, wcols], wgu.at[h, 0, 0], wl_sem.at[0]).start()
            pltpu.make_async_copy(wu_ref.at[:, :, wcols], wgu.at[h, 1, 0], wl_sem.at[0]).start()
            pltpu.make_async_copy(wd_ref.at[:, :, wcols], wdn.at[h, 0], wl_sem.at[1]).start()

        for copy in inputs:
            copy.wait()
        lane = lax.broadcasted_iota(jnp.int32, (2, META), 1)
        row = lax.broadcasted_iota(jnp.int32, (2, META), 0)
        gates = jnp.zeros((2, META), jnp.int32)
        for k in range(ids_ref.shape[1]):
            gates += jnp.where((lane == idsv[0, k]) & (row == 0), gatesv[0, k], 0)
        tsend[:, 0:META] = gates.astype(F32).astype(BF16)
        tok = tokv[...].astype(F32)
        tsend[:, META:] = jnp.concatenate([tok[:, :half], tok[:, half:]], axis=0).astype(BF16)

        @pl.when(lead)
        def _():
            t1[y * 2 + 1] = tsend[...]

    with scope("bar"):
        pl.semaphore_wait(barrier, ny + jnp.where(lead, ny - 1 + nx - 1 + 2, 0))

    with scope("ypush"):
        for q in range(CHUNKS):
            for v in ys:
                push(tsend.at[:, part(q)], t1.at[y * 2 + c, :, part(q)], s1, r1.at[q], at_y(v, 1))

            @pl.when(jnp.logical_not(lead))
            def _():
                push(tsend.at[:, part(q)], t1.at[y * 2 + c, :, part(q)], s0, r1.at[q], partner)

        for h in range(2):
            wcols = pl.ds(h * half, half)
            push(wg_ref.at[:, :, wcols], wgu.at[h, 0, 1], ws_sem.at[0], wr_sem.at[0], partner)
            push(wu_ref.at[:, :, wcols], wgu.at[h, 1, 1], ws_sem.at[0], wr_sem.at[0], partner)
            push(wd_ref.at[:, :, wcols], wdn.at[h, 1], ws_sem.at[1], wr_sem.at[1], partner)

    cells = nx * ny * 2

    def order(i):
        return ((i // 2) % ny) * nx + i // (2 * ny)

    def picker(col, side):
        i0 = lax.broadcasted_iota(jnp.int32, (cells, cells), 0)
        i1 = lax.broadcasted_iota(jnp.int32, (cells, cells), 1)
        same = ones(i0 // 2 == i1 // 2)
        own = ones(lax.broadcasted_iota(jnp.int32, (rows, META), 1) // 2 == n)
        meta = t2[:, col, :, 0:META].reshape(cells, META)
        if side == 0:
            total = lax.dot_general(own, meta, NT, preferred_element_type=F32)
            hit = ones(total > 0)
            rank = jnp.dot(hit, ones(order(i0) < order(i1)), preferred_element_type=F32)
            hit = jnp.dot(hit, same, preferred_element_type=F32)
            shape = (rows, cells)
        else:
            total = lax.dot_general(meta, own, NT, preferred_element_type=F32)
            hit = ones(total > 0)
            rank = jnp.dot(ones(order(i1) < order(i0)), hit, preferred_element_type=F32)
            hit = jnp.dot(same, hit, preferred_element_type=F32)
            shape = (cells, rows)
        r = lax.broadcasted_iota(jnp.int32, shape, side)
        i = lax.broadcasted_iota(jnp.int32, shape, 1 - side)
        return ones((hit > 0) & (rank == (r // 2).astype(F32)) & (r % 2 == i % 2))

    def weights_here():
        await_bytes(wgu.at[:, :, 0], wl_sem.at[0])
        await_bytes(wdn.at[:, 0], wl_sem.at[1])
        await_bytes(wgu.at[:, :, 1], wr_sem.at[0])
        await_bytes(wdn.at[:, 1], wr_sem.at[1])

    def gate_up(start, blocks, q):
        count = blocks * 2 * rows
        piece = xbuf[start : start + blocks, :, :, pl.ds(d_off[q], width)].reshape(count, width)
        for h in range(2):
            w = wgu[h, :, :, :, :, cols(q)].reshape(2 * units, width)
            v = lax.dot_general(piece, w, NT, preferred_element_type=F32)
            for k in range(2):
                if q == 0:
                    zbuf[h, k, 0:count] = v[:, k * units : (k + 1) * units]
                else:
                    zbuf[h, k, 0:count] += v[:, k * units : (k + 1) * units]

    def activations(start, blocks):
        count = blocks * 2 * rows
        lane = lax.broadcasted_iota(jnp.int32, (META, units), 0)
        unit = lax.broadcasted_iota(jnp.int32, (META, units), 1)
        chosen = ones(lane == 2 * n + (unit // ffl) % 2)
        gate_rows = xbuf[start : start + blocks, :, :, 0:META].reshape(count, META)
        hbuf[0, 0:count] = jnp.dot(gate_rows, chosen, preferred_element_type=F32)
        even, odd = pl.ds(0, count // 2, 2), pl.ds(1, count // 2, 2)
        gate_act = zbuf[0, 0, even, :] + zbuf[1, 0, odd, :]
        up_act = zbuf[0, 1, even, :] + zbuf[1, 1, odd, :]
        scale = hbuf[0, even, :] / 8.0
        hidden = gate_act / (1.0 + jnp.exp(-gate_act)) * up_act * scale
        none = jnp.zeros_like(hidden)
        hbuf[0, even, :] = hidden
        hbuf[1, even, :] = none
        hbuf[0, odd, :] = none
        hbuf[1, odd, :] = hidden
        return jnp.concatenate([hbuf[0, 0:count], hbuf[1, 0:count]], axis=1).astype(BF16)

    def project(hidden, q):
        w = wdn[:, :, :, :, cols(q)].reshape(2 * units, width)
        return jnp.dot(hidden, w, preferred_element_type=F32)

    def slot(direction, step):
        return direction * hz + step - 1

    @pl.when(jnp.logical_not(lead))
    def _():
        with scope("s_wait"):
            weights_here()
            await_bytes(xbuf.at[0:near], rx)
        with scope("s_gateup"):
            for q in range(CHUNKS):
                gate_up(0, near, q)
        with scope("s_act"):
            hidden = activations(0, near)
        with scope("s_down"):
            for q in range(CHUNKS):
                v = project(hidden, q)
                pnear[:, :, :, cols(q)] = v.reshape(near, 2, rows, width).astype(BF16)
            for s in range(hz - 2, 0, -1):
                for b in (going_down(s), going_up(s)):
                    push(pnear.at[b], pnear.at[b], sp, rp.at[s], partner)
            push(pnear.at[0], pnear.at[0], sp, rp.at[0], partner)

    @pl.when(lead)
    def _():
        with scope("xstage"):
            for q in range(CHUNKS):
                await_bytes(t1.at[pl.ds(0, 2 * ny - 1), :, part(q)], r1.at[q])
                for v in range(ny):
                    for col in range(2):
                        t2[x, col, 2 * v : 2 * v + 2, part(q)] = t1[2 * v + col, :, part(q)]
                for v in xs:
                    own = t2.at[x, :, :, part(q)]
                    push(own, own, s2, r2.at[q], at_x(v))

        with scope("pack"):
            pickers = None
            for q in range(CHUNKS):
                await_bytes(t2.at[pl.ds(0, nx - 1), :, :, part(q)], r2.at[q])
                if q == 0:
                    pickers = [picker(col, 0) for col in range(2)]
                for col in range(2):
                    field = t2[:, col, :, part(q)].reshape(cells, lens[q])
                    picked = jnp.dot(pickers[col], field, preferred_element_type=F32)
                    xbuf[0, col, :, part(q)] = picked.astype(BF16)
                own = xbuf.at[0, :, :, part(q)]
                push(own, xbuf.at[going_up(1), :, :, part(q)], sa, ra.at[slot(0, 1), q], up)
                push(own, xbuf.at[going_down(1), :, :, part(q)], sa, ra.at[slot(1, 1), q], down)
                push(own, own, sx, rx, partner)
            weights_here()

        with scope("ring"):
            for s in range(1, hz + 1):
                for q in range(CHUNKS):
                    b = going_up(s)
                    block = xbuf.at[b, :, :, part(q)]
                    await_bytes(block, ra.at[slot(0, s), q])
                    if s < hz:
                        push(block, xbuf.at[going_up(s + 1), :, :, part(q)], sa, ra.at[slot(0, s + 1), q], up)
                    if b < near:
                        push(block, block, sx, rx, partner)
                    if s < hz:
                        b = going_down(s)
                        block = xbuf.at[b, :, :, part(q)]
                        await_bytes(block, ra.at[slot(1, s), q])
                        if s < hz - 1:
                            push(block, xbuf.at[going_down(s + 1), :, :, part(q)], sa, ra.at[slot(1, s + 1), q], down)
                        if b < near:
                            push(block, block, sx, rx, partner)
                    else:
                        gate_up(near, far, q)
        with scope("act"):
            hidden = activations(near, far)

        def onward(direction, s, q, value, device):
            i = slot(direction, s)
            if s > 1:
                await_bytes(rrecv.at[i - 1, :, :, cols(q)], rs.at[i - 1, q])
                value = value.astype(F32) + rrecv[i - 1, :, :, cols(q)].astype(F32)
            rsend[i, :, :, cols(q)] = value.astype(BF16)
            push(rsend.at[i, :, :, cols(q)], rrecv.at[i, :, :, cols(q)], ss, rs.at[i, q], device)

        with scope("rs1"):
            for q in range(CHUNKS):
                v = project(hidden, q).reshape(far, 2, rows, width)
                pfar[:, :, cols(q)] = v[2]
                onward(0, 1, q, v[1], up)
                onward(1, 1, q, v[0], down)
        with scope("rs"):
            for s in range(2, hz + 1):
                above, below = hz + 1 - s, hz - s
                if s < hz:
                    await_bytes(pnear.at[0:2], rp.at[below])
                for q in range(CHUNKS):
                    value = pfar[:, :, cols(q)] if s == 2 else pnear[going_down(above), :, :, cols(q)]
                    onward(0, s, q, value, up)
                    if s < hz:
                        onward(1, s, q, pnear[going_up(below), :, :, cols(q)], down)

        with scope("retx"):
            pickers = [picker(col, 1) for col in range(2)]
            await_bytes(pnear.at[0], rp.at[0])
            for q in range(CHUNKS):
                one, two = slot(0, hz), slot(1, hz - 1)
                await_bytes(rrecv.at[two, :, :, cols(q)], rs.at[two, q])
                await_bytes(rrecv.at[one, :, :, cols(q)], rs.at[one, q])
                total = pnear[0, :, :, cols(q)].astype(F32) + rrecv[one, :, :, cols(q)].astype(F32)
                total = (total + rrecv[two, :, :, cols(q)].astype(F32)).astype(BF16)
                for col in range(2):
                    placed = jnp.dot(pickers[col], total[col], preferred_element_type=F32)
                    ysend[:, col, :, cols(q)] = placed.astype(BF16).reshape(nx, 2 * ny, width)
                for v in xs:
                    push(ysend.at[v, :, :, cols(q)], yrecv.at[x, :, :, cols(q)], s3, r3.at[q], at_x(v))
        with scope("rety"):
            for q in range(CHUNKS):
                await_bytes(yrecv.at[pl.ds(0, nx - 1), :, :, cols(q)], r3.at[q])
                total = ysend[x, :, :, cols(q)].astype(F32)
                for v in xs:
                    total += yrecv[v, :, :, cols(q)].astype(F32)
                total = total.astype(BF16)
                for v in range(ny):
                    for col in range(2):
                        fsend[v, col, :, cols(q)] = total[col, 2 * v : 2 * v + 2, :]
                for v in ys:
                    for col in range(2):
                        push(fsend.at[v, col, :, cols(q)], frecv.at[y, :, cols(q)], s4, r4.at[q], at_y(v, col))
                push(fsend.at[y, 0, :, cols(q)], frecv.at[y, :, cols(q)], s0, r4.at[q], partner)
                frecv[y, :, cols(q)] = fsend[y, 1, :, cols(q)]

    with scope("final"):
        for q in range(CHUNKS):
            @pl.when(lead)
            def _():
                await_bytes(frecv.at[0 : ny - 1, :, cols(q)], r4.at[q])

            @pl.when(jnp.logical_not(lead))
            def _():
                await_bytes(frecv.at[:, :, cols(q)], r4.at[q])

            total = frecv[0, :, cols(q)].astype(F32)
            for v in range(1, ny):
                total += frecv[v, :, cols(q)].astype(F32)
            total = total.astype(BF16)
            out_ref[0:1, cols(q)] = total[0:1, :]
            out_ref[0:1, pl.ds(half + q * width, width)] = total[1:2, :]

    with scope("drain"):
        await_bytes(t1.at[0 : ny - 1], s1)
        await_bytes(wgu.at[:, :, 1], ws_sem.at[0])
        await_bytes(wdn.at[:, 1], ws_sem.at[1])

        @pl.when(jnp.logical_not(lead))
        def _():
            await_bytes(tsend, s0)
            await_bytes(pnear, sp)

        @pl.when(lead)
        def _():
            await_bytes(t2.at[0 : nx - 1], s2)
            await_bytes(xbuf.at[0 : nz - 1], sa)
            await_bytes(xbuf.at[0:near], sx)
            await_bytes(rsend, ss)
            await_bytes(yrecv.at[0 : nx - 1], s3)
            await_bytes(fsend.at[0 : ny - 1], s4)
            await_bytes(frecv.at[0], s0)


def solution(mesh):
    nodes, locals_ = mesh.shape["node"], mesh.shape["local"]
    nx = min(NX, nodes)
    ny, nz = nodes // nx, locals_ // 2
    hz = nz // 2
    near = 1 + 2 * (hz - 2)

    def on_device(tokens, w_gate, w_up, w_down, expert_ids, gate_ints):
        model_width = tokens.shape[1]
        half = model_width // 2
        exp_node, ffl = w_gate.shape[0], w_gate.shape[1]
        units = 2 * exp_node * ffl
        rows = 2 * CAP
        sem = pltpu.SemaphoreType.DMA
        one = sem(())
        any_space = pl.BlockSpec(memory_space=pl.ANY)
        vmem = pl.BlockSpec(memory_space=pltpu.VMEM)
        return pl.pallas_call(
            functools.partial(layer_kernel, nx, ny, nz),
            out_shape=jax.ShapeDtypeStruct((1, model_width), BF16),
            in_specs=[any_space] * 6,
            out_specs=vmem,
            scratch_shapes=[
                pltpu.VMEM((1, model_width), BF16),
                pltpu.SMEM(expert_ids.shape, jnp.int32),
                pltpu.SMEM(gate_ints.shape, jnp.int32),
                pltpu.VMEM((2, META + half), BF16),
                pltpu.VMEM((2 * ny, 2, META + half), BF16),
                pltpu.VMEM((nx, 2, 2 * ny, META + half), BF16),
                pltpu.VMEM((nz, 2, rows, META + half), BF16),
                pltpu.VMEM((2, 2, 2, exp_node, ffl, half), BF16),
                pltpu.VMEM((2, 2, exp_node, ffl, half), BF16),
                pltpu.VMEM((2, 2, near * 2 * rows, units), F32),
                pltpu.VMEM((2, near * 2 * rows, units), F32),
                pltpu.VMEM((2, rows, half), F32),
                pltpu.VMEM((near, 2, rows, half), BF16),
                pltpu.VMEM((nz - 1, 2, rows, half), BF16),
                pltpu.VMEM((nz - 1, 2, rows, half), BF16),
                pltpu.VMEM((nx, 2, 2 * ny, half), BF16),
                pltpu.VMEM((nx, 2, 2 * ny, half), BF16),
                pltpu.VMEM((ny, 2, 2, half), BF16),
                pltpu.VMEM((ny, 2, half), BF16),
                sem((3,)), sem((2,)), sem((2,)), sem((2,)),
                one, one, sem((CHUNKS,)), one, sem((CHUNKS,)),
                one, sem((nz - 1, CHUNKS)), one, one, one, sem((hz - 1,)),
                one, sem((nz - 1, CHUNKS)), one, sem((CHUNKS,)), one, sem((CHUNKS,)),
            ],
            compiler_params=pltpu.CompilerParams(
                collective_id=0, has_side_effects=True, vmem_limit_bytes=60 * 1024 * 1024
            ),
            name="layer",
        )(tokens, w_gate, w_up, w_down, expert_ids, gate_ints)

    both = P(("node", "local"), None)
    weights = P("node", "local", None)
    return jax.shard_map(
        on_device, mesh=mesh,
        in_specs=(both, weights, weights, weights, both, both),
        out_specs=both, check_vma=False,
    )
```

time: 276 us -> 92.2 us (0.33)
  the two profiles are of different devices: /device:TPU:8 before, /device:TPU:1 now
where the time goes in v2:
time: 92.2 us; the launch traced here: 91.9 us
  Pallas kernels  90.5 us (98%)
  local copies, waits for them, and re-layouts  1.39 us (2%)
    pallas_call x1, Pallas kernels, on_device(): pl.pallas_call(functools.partial(layer_kernel, nx, ny, nz), out_shape=jax...  90.5 us

profile of v2, /device:TPU:1, one launch (start us, length us, event | category | flops | bytes accessed | tf_op | source)
XLA Modules:
  0.0 91.9 jit_solution(6141402523640424127)
XLA Ops:
  0.0 90.5 %layer.1 = bf16[1,7168]{1,0:T(2,128)(2,1)} custom-call(bf16[1,7168]{1,0:T(2,128)(2,1)} %tok_ref.1, bf16[2,32,7168]{2,1,0:T(8,128)(2,1)} %wg_ref.1, bf16[2,32,7168]{2,1,0:T(8,128)(2,1)} %wu_ref.1, bf16[2,32,7168]{2,1,0:T(8,128)(2,1)} %wd_ref.1, s32[1,8]{1,0:T(1,128)} %ids_ref.1, s32[1,8]{1,0:T(1,128)} %gates_ref.1), custom_call_target="tpu_custom_call" | custom-call | tf_op jit(solution)/shard_map/layer/pallas_call | solution.py:399
  90.6 1.4 %copy.8 = bf16[1,7168]{1,0:T(2,128)(2,1)} copy(bf16[1,7168]{1,0:T(2,128)(2,1)} %layer.1) | data formatting | bytes 28672

commit v3 on v2

--- a/solution.py
+++ b/solution.py
@@ -26,9 +26,10 @@
     nx, ny, nz,
     tok_ref, wg_ref, wu_ref, wd_ref, ids_ref, gates_ref,
     out_ref,
-    tokv, idsv, gatesv, tsend, t1, t2, xbuf, wgu, wdn, zbuf, hbuf, pfar, pnear, rsend, rrecv,
-    ysend, yrecv, fsend, frecv,
+    tokv, idsv, gatesv, tsend, t1, t2, xbuf, wgu, wdn, zbuf, hbuf, pnear, rsend, rrecv,
+    ysend, yrecv, fsend, frecv, ftok, ft1, ft2, fxs, fxr, fys, fyr, fzs, fin,
     in_sem, wl_sem, ws_sem, wr_sem, s0, s1, r1, s2, r2, sa, ra, sx, rx, sp, rp, ss, rs, s3, r3, s4, r4,
+    fs, fr, ready,
 ):
     half = wgu.shape[-1]
     width = half // CHUNKS
@@ -45,8 +46,8 @@
     z, c = l // 2, lax.rem(l, 2)
     lead = c == 1
 
-    def at_x(v):
-        return (y * nx + v, z * 2 + 1)
+    def at_x(v, core=1):
+        return (y * nx + v, z * 2 + core)
 
     def at_y(v, core):
         return (v * nx + x, z * 2 + core)
@@ -57,14 +58,20 @@
     xs = [lax.rem(x + d, nx) for d in range(1, nx)]
     ys = [lax.rem(y + d, ny) for d in range(1, ny)]
 
-    near = 1 + 2 * (hz - 2)
-    far = 3
+    steps = hz - 1
+    near = 2 * steps - 1
+    opposite = near + 2
 
     def going_up(s):
-        return s if s <= hz - 2 else near + s - (hz - 1)
+        return s if s < steps else near
 
     def going_down(s):
-        return hz - 2 + s if s <= hz - 2 else near + 2
+        return steps - 1 + s if s < steps else near + 1
+
+    early = z < hz
+
+    def across(core):
+        return (n, lax.rem(z + hz, nz) * 2 + core)
 
     def push(src, dst, send, recv, device):
         pltpu.make_async_remote_copy(
@@ -89,15 +96,22 @@
         signal(barrier, partner)
         for v in ys:
             signal(barrier, at_y(v, 1))
+            signal(barrier, at_y(v, 0))
+        for v in xs:
+            signal(barrier, at_x(v, c))
 
         @pl.when(lead)
         def _():
-            for v in ys:
-                signal(barrier, at_y(v, 0))
-            for v in xs:
-                signal(barrier, at_x(v))
             signal(barrier, up)
             signal(barrier, down)
+
+        @pl.when(early)
+        def _():
+            signal(barrier, across(0))
+
+            @pl.when(jnp.logical_not(lead))
+            def _():
+                signal(barrier, across(1))
 
         inputs = [
             pltpu.make_async_copy(tok_ref, tokv, in_sem.at[0]),
@@ -127,8 +141,17 @@
         def _():
             t1[y * 2 + 1] = tsend[...]
 
+        @pl.when(jnp.logical_not(lead))
+        def _():
+            ftok[0] = tsend[...]
+
     with scope("bar"):
-        pl.semaphore_wait(barrier, ny + jnp.where(lead, ny - 1 + nx - 1 + 2, 0))
+        count = 1 + 2 * (ny - 1) + nx - 1 + 2 * c + (z // hz) * (2 - c)
+        pl.semaphore_wait(barrier, count)
+
+        @pl.when(jnp.logical_not(early))
+        def _():
+            signal(ready, across(0))
 
     with scope("ypush"):
         for q in range(CHUNKS):
@@ -138,6 +161,10 @@
             @pl.when(jnp.logical_not(lead))
             def _():
                 push(tsend.at[:, part(q)], t1.at[y * 2 + c, :, part(q)], s0, r1.at[q], partner)
+
+        @pl.when(lead)
+        def _():
+            push(tsend, ftok.at[1], fs.at[0], fr.at[6], partner)
 
         for h in range(2):
             wcols = pl.ds(h * half, half)
@@ -150,12 +177,12 @@
     def order(i):
         return ((i // 2) % ny) * nx + i // (2 * ny)
 
-    def picker(col, side):
+    def picker(field, col, side):
         i0 = lax.broadcasted_iota(jnp.int32, (cells, cells), 0)
         i1 = lax.broadcasted_iota(jnp.int32, (cells, cells), 1)
         same = ones(i0 // 2 == i1 // 2)
         own = ones(lax.broadcasted_iota(jnp.int32, (rows, META), 1) // 2 == n)
-        meta = t2[:, col, :, 0:META].reshape(cells, META)
+        meta = field[:, col, :, 0:META].reshape(cells, META)
         if side == 0:
             total = lax.dot_general(own, meta, NT, preferred_element_type=F32)
             hit = ones(total > 0)
@@ -214,10 +241,28 @@
         return jnp.dot(hidden, w, preferred_element_type=F32)
 
     def slot(direction, step):
-        return direction * hz + step - 1
+        return direction * steps + step - 1
 
     @pl.when(jnp.logical_not(lead))
     def _():
+        with scope("f_token"):
+            @pl.when(early)
+            def _():
+                pl.semaphore_wait(ready, 2)
+
+            await_bytes(ftok.at[1], fr.at[6])
+            push(ftok, ft1.at[y], fs.at[0], fr.at[0], across(0))
+        with scope("f_y"):
+            await_bytes(ft1.at[y], fr.at[0])
+            for v in ys:
+                push(ft1.at[y], ft1.at[y], fs.at[1], fr.at[1], at_y(v, 0))
+        with scope("f_x"):
+            await_bytes(ft1.at[0 : ny - 1], fr.at[1])
+            for v in range(ny):
+                for col in range(2):
+                    ft2[x, col, 2 * v : 2 * v + 2] = ft1[v, col]
+            for v in xs:
+                push(ft2.at[x], ft2.at[x], fs.at[2], fr.at[2], at_x(v, 0))
         with scope("s_wait"):
             weights_here()
             await_bytes(xbuf.at[0:near], rx)
@@ -230,10 +275,51 @@
             for q in range(CHUNKS):
                 v = project(hidden, q)
                 pnear[:, :, :, cols(q)] = v.reshape(near, 2, rows, width).astype(BF16)
-            for s in range(hz - 2, 0, -1):
+            for s in range(steps - 1, 0, -1):
                 for b in (going_down(s), going_up(s)):
                     push(pnear.at[b], pnear.at[b], sp, rp.at[s], partner)
             push(pnear.at[0], pnear.at[0], sp, rp.at[0], partner)
+        with scope("f_pack"):
+            await_bytes(ft2.at[0 : nx - 1], fr.at[2])
+            pickers = [picker(ft2, col, 0) for col in range(2)]
+            for col in range(2):
+                for q in range(CHUNKS):
+                    field = ft2[:, col, :, part(q)].reshape(cells, lens[q])
+                    picked = jnp.dot(pickers[col], field, preferred_element_type=F32)
+                    xbuf[opposite, col, :, part(q)] = picked.astype(BF16)
+            for q in range(CHUNKS):
+                gate_up(opposite, 1, q)
+            hidden = activations(opposite, 1)
+        with scope("f_retx"):
+            pickers = [picker(ft2, col, 1) for col in range(2)]
+            for q in range(CHUNKS):
+                v = project(hidden, q).astype(BF16).reshape(2, rows, width)
+                for col in range(2):
+                    placed = jnp.dot(pickers[col], v[col], preferred_element_type=F32)
+                    fxs[:, col, :, cols(q)] = placed.astype(BF16).reshape(nx, 2 * ny, width)
+            for v in xs:
+                push(fxs.at[v], fxr.at[x], fs.at[3], fr.at[3], at_x(v, 0))
+        with scope("f_rety"):
+            await_bytes(fxr.at[0 : nx - 1], fr.at[3])
+            for q in range(CHUNKS):
+                total = fxs[x, :, :, cols(q)].astype(F32)
+                for v in xs:
+                    total += fxr[v, :, :, cols(q)].astype(F32)
+                total = total.astype(BF16)
+                for v in range(ny):
+                    for col in range(2):
+                        fys[v, col, :, cols(q)] = total[col, 2 * v : 2 * v + 2, :]
+            for v in ys:
+                push(fys.at[v], fyr.at[y], fs.at[4], fr.at[4], at_y(v, 0))
+        with scope("f_retz"):
+            await_bytes(fyr.at[0 : ny - 1], fr.at[4])
+            for q in range(CHUNKS):
+                total = fys[y, :, :, cols(q)].astype(F32)
+                for v in ys:
+                    total += fyr[v, :, :, cols(q)].astype(F32)
+                fzs[:, :, cols(q)] = total.astype(BF16)
+            for core in range(2):
+                push(fzs.at[core], fin, fs.at[5], fr.at[5], across(core))
 
     @pl.when(lead)
     def _():
@@ -252,7 +338,7 @@
             for q in range(CHUNKS):
                 await_bytes(t2.at[pl.ds(0, nx - 1), :, :, part(q)], r2.at[q])
                 if q == 0:
-                    pickers = [picker(col, 0) for col in range(2)]
+                    pickers = [picker(t2, col, 0) for col in range(2)]
                 for col in range(2):
                     field = t2[:, col, :, part(q)].reshape(cells, lens[q])
                     picked = jnp.dot(pickers[col], field, preferred_element_type=F32)
@@ -264,58 +350,48 @@
             weights_here()
 
         with scope("ring"):
-            for s in range(1, hz + 1):
+            for s in range(1, steps + 1):
                 for q in range(CHUNKS):
-                    b = going_up(s)
-                    block = xbuf.at[b, :, :, part(q)]
-                    await_bytes(block, ra.at[slot(0, s), q])
-                    if s < hz:
-                        push(block, xbuf.at[going_up(s + 1), :, :, part(q)], sa, ra.at[slot(0, s + 1), q], up)
-                    if b < near:
-                        push(block, block, sx, rx, partner)
-                    if s < hz:
-                        b = going_down(s)
+                    for direction, b, later, device in (
+                        (0, going_up(s), going_up(s + 1), up),
+                        (1, going_down(s), going_down(s + 1), down),
+                    ):
                         block = xbuf.at[b, :, :, part(q)]
-                        await_bytes(block, ra.at[slot(1, s), q])
-                        if s < hz - 1:
-                            push(block, xbuf.at[going_down(s + 1), :, :, part(q)], sa, ra.at[slot(1, s + 1), q], down)
-                        if b < near:
+                        await_bytes(block, ra.at[slot(direction, s), q])
+                        if s < steps:
+                            push(block, xbuf.at[later, :, :, part(q)], sa, ra.at[slot(direction, s + 1), q], device)
                             push(block, block, sx, rx, partner)
-                    else:
-                        gate_up(near, far, q)
+                    if s == steps:
+                        gate_up(near, 2, q)
         with scope("act"):
-            hidden = activations(near, far)
+            hidden = activations(near, 2)
 
         def onward(direction, s, q, value, device):
             i = slot(direction, s)
             if s > 1:
                 await_bytes(rrecv.at[i - 1, :, :, cols(q)], rs.at[i - 1, q])
-                value = value.astype(F32) + rrecv[i - 1, :, :, cols(q)].astype(F32)
-            rsend[i, :, :, cols(q)] = value.astype(BF16)
+                value = value + rrecv[i - 1, :, :, cols(q)]
+            rsend[i, :, :, cols(q)] = value
             push(rsend.at[i, :, :, cols(q)], rrecv.at[i, :, :, cols(q)], ss, rs.at[i, q], device)
 
         with scope("rs1"):
             for q in range(CHUNKS):
-                v = project(hidden, q).reshape(far, 2, rows, width)
-                pfar[:, :, cols(q)] = v[2]
+                v = project(hidden, q).astype(BF16).reshape(2, 2, rows, width)
                 onward(0, 1, q, v[1], up)
                 onward(1, 1, q, v[0], down)
         with scope("rs"):
-            for s in range(2, hz + 1):
-                above, below = hz + 1 - s, hz - s
-                if s < hz:
-                    await_bytes(pnear.at[0:2], rp.at[below])
+            pickers = [picker(t2, col, 1) for col in range(2)]
+            for s in range(2, steps + 1):
+                at = steps + 1 - s
+                await_bytes(pnear.at[0:2], rp.at[at])
                 for q in range(CHUNKS):
-                    value = pfar[:, :, cols(q)] if s == 2 else pnear[going_down(above), :, :, cols(q)]
-                    onward(0, s, q, value, up)
-                    if s < hz:
-                        onward(1, s, q, pnear[going_up(below), :, :, cols(q)], down)
+                    onward(0, s, q, pnear[going_down(at), :, :, cols(q)], up)
+                    onward(1, s, q, pnear[going_up(at), :, :, cols(q)], down)
 
         with scope("retx"):
-            pickers = [picker(col, 1) for col in range(2)]
             await_bytes(pnear.at[0], rp.at[0])
             for q in range(CHUNKS):
-                one, two = slot(0, hz), slot(1, hz - 1)
+                one, two = slot(0, steps), slot(1, steps)
                 await_bytes(rrecv.at[two, :, :, cols(q)], rs.at[two, q])
                 await_bytes(rrecv.at[one, :, :, cols(q)], rs.at[one, q])
                 total = pnear[0, :, :, cols(q)].astype(F32) + rrecv[one, :, :, cols(q)].astype(F32)
@@ -351,8 +427,10 @@
             def _():
                 await_bytes(frecv.at[:, :, cols(q)], r4.at[q])
 
-            total = frecv[0, :, cols(q)].astype(F32)
-            for v in range(1, ny):
+            if q == 0:
+                await_bytes(fin, fr.at[5])
+            total = fin[:, cols(q)].astype(F32)
+            for v in range(ny):
                 total += frecv[v, :, cols(q)].astype(F32)
             total = total.astype(BF16)
             out_ref[0:1, cols(q)] = total[0:1, :]
@@ -367,16 +445,23 @@
         def _():
             await_bytes(tsend, s0)
             await_bytes(pnear, sp)
+            await_bytes(ftok, fs.at[0])
+            await_bytes(ft1.at[0 : ny - 1], fs.at[1])
+            await_bytes(ft2.at[0 : nx - 1], fs.at[2])
+            await_bytes(fxs.at[0 : nx - 1], fs.at[3])
+            await_bytes(fys.at[0 : ny - 1], fs.at[4])
+            await_bytes(fzs, fs.at[5])
 
         @pl.when(lead)
         def _():
             await_bytes(t2.at[0 : nx - 1], s2)
-            await_bytes(xbuf.at[0 : nz - 1], sa)
+            await_bytes(xbuf.at[0 : 2 * steps], sa)
             await_bytes(xbuf.at[0:near], sx)
             await_bytes(rsend, ss)
             await_bytes(yrecv.at[0 : nx - 1], s3)
             await_bytes(fsend.at[0 : ny - 1], s4)
             await_bytes(frecv.at[0], s0)
+            await_bytes(tsend, fs.at[0])
 
 
 def solution(mesh):
@@ -384,7 +469,8 @@
     nx = min(NX, nodes)
     ny, nz = nodes // nx, locals_ // 2
     hz = nz // 2
-    near = 1 + 2 * (hz - 2)
+    steps = hz - 1
+    near = 2 * steps - 1
 
     def on_device(tokens, w_gate, w_up, w_down, expert_ids, gate_ints):
         model_width = tokens.shape[1]
@@ -413,18 +499,27 @@
                 pltpu.VMEM((2, 2, exp_node, ffl, half), BF16),
                 pltpu.VMEM((2, 2, near * 2 * rows, units), F32),
                 pltpu.VMEM((2, near * 2 * rows, units), F32),
-                pltpu.VMEM((2, rows, half), F32),
                 pltpu.VMEM((near, 2, rows, half), BF16),
-                pltpu.VMEM((nz - 1, 2, rows, half), BF16),
-                pltpu.VMEM((nz - 1, 2, rows, half), BF16),
+                pltpu.VMEM((2 * steps, 2, rows, half), BF16),
+                pltpu.VMEM((2 * steps, 2, rows, half), BF16),
                 pltpu.VMEM((nx, 2, 2 * ny, half), BF16),
                 pltpu.VMEM((nx, 2, 2 * ny, half), BF16),
                 pltpu.VMEM((ny, 2, 2, half), BF16),
                 pltpu.VMEM((ny, 2, half), BF16),
+                pltpu.VMEM((2, 2, META + half), BF16),
+                pltpu.VMEM((ny, 2, 2, META + half), BF16),
+                pltpu.VMEM((nx, 2, 2 * ny, META + half), BF16),
+                pltpu.VMEM((nx, 2, 2 * ny, half), BF16),
+                pltpu.VMEM((nx, 2, 2 * ny, half), BF16),
+                pltpu.VMEM((ny, 2, 2, half), BF16),
+                pltpu.VMEM((ny, 2, 2, half), BF16),
+                pltpu.VMEM((2, 2, half), BF16),
+                pltpu.VMEM((2, half), BF16),
                 sem((3,)), sem((2,)), sem((2,)), sem((2,)),
                 one, one, sem((CHUNKS,)), one, sem((CHUNKS,)),
-                one, sem((nz - 1, CHUNKS)), one, one, one, sem((hz - 1,)),
-                one, sem((nz - 1, CHUNKS)), one, sem((CHUNKS,)), one, sem((CHUNKS,)),
+                one, sem((2 * steps, CHUNKS)), one, one, one, sem((steps,)),
+                one, sem((2 * steps, CHUNKS)), one, sem((CHUNKS,)), one, sem((CHUNKS,)),
+                sem((6,)), sem((7,)), pltpu.SemaphoreType.REGULAR,
             ],
             compiler_params=pltpu.CompilerParams(
                 collective_id=0, has_side_effects=True, vmem_limit_bytes=60 * 1024 * 1024

time: 92.2 us -> 89 us (0.965)
  Pallas kernels: 90.5 us -> 87.4 us
    pallas_call x1, Pallas kernels: 90.5 us -> 87.4 us  [on_device(): pl.pallas_call(functools.partial(layer_kernel, nx, ny, nz), out_shape=jax...]
where the time goes in v3:
time: 89 us; the launch traced here: 88.8 us
  Pallas kernels  87.4 us (98%)
  local copies, waits for them, and re-layouts  1.39 us (2%)
    pallas_call x1, Pallas kernels, on_device(): pl.pallas_call(functools.partial(layer_kernel, nx, ny, nz), out_shape=jax...  87.4 us

profile of v3, /device:TPU:1, one launch (start us, length us, event | category | flops | bytes accessed | tf_op | source)
XLA Modules:
  0.0 88.8 jit_solution(15763972435043615520)
XLA Ops:
  0.0 87.4 %layer.1 = bf16[1,7168]{1,0:T(2,128)(2,1)} custom-call(bf16[1,7168]{1,0:T(2,128)(2,1)} %tok_ref.1, bf16[2,32,7168]{2,1,0:T(8,128)(2,1)} %wg_ref.1, bf16[2,32,7168]{2,1,0:T(8,128)(2,1)} %wu_ref.1, bf16[2,32,7168]{2,1,0:T(8,128)(2,1)} %wd_ref.1, s32[1,8]{1,0:T(1,128)} %ids_ref.1, s32[1,8]{1,0:T(1,128)} %gates_ref.1), custom_call_target="tpu_custom_call" | custom-call | tf_op jit(solution)/shard_map/layer/pallas_call | solution.py:485
  87.4 1.4 %copy.8 = bf16[1,7168]{1,0:T(2,128)(2,1)} copy(bf16[1,7168]{1,0:T(2,128)(2,1)} %layer.1) | data formatting | bytes 28672

commit v4 on v3

--- a/solution.py
+++ b/solution.py
@@ -10,6 +10,7 @@
 CAP = 8
 NX = 4
 CHUNKS = 7
+OTHER = 2
 META = 128
 BF16 = jnp.bfloat16
 F32 = jnp.float32
@@ -27,9 +28,9 @@
     tok_ref, wg_ref, wu_ref, wd_ref, ids_ref, gates_ref,
     out_ref,
     tokv, idsv, gatesv, tsend, t1, t2, xbuf, wgu, wdn, zbuf, hbuf, pnear, rsend, rrecv,
-    ysend, yrecv, fsend, frecv, ftok, ft1, ft2, fxs, fxr, fys, fyr, fzs, fin,
-    in_sem, wl_sem, ws_sem, wr_sem, s0, s1, r1, s2, r2, sa, ra, sx, rx, sp, rp, ss, rs, s3, r3, s4, r4,
-    fs, fr, ready,
+    ysend, yrecv, fsend, frecv, ftok, ft1, ft2, fxs, fxr, fys, fyr, fzs, fin, a1, b1, c1, c2, e1, e2,
+    in_sem, wl_sem, ws_sem, wr_sem, s0, s1, r1, s2, r2, sa, ra, sx, rx, sp, rp, ss, s3, r3, s4, r4,
+    fs, fr, ready, so,
 ):
     half = wgu.shape[-1]
     width = half // CHUNKS
@@ -63,10 +64,10 @@
     opposite = near + 2
 
     def going_up(s):
-        return s if s < steps else near
+        return 2 * s - 1
 
     def going_down(s):
-        return steps - 1 + s if s < steps else near + 1
+        return 2 * s
 
     early = z < hz
 
@@ -90,6 +91,15 @@
 
     def cols(q):
         return pl.ds(q * width, width)
+
+    main, other = range(CHUNKS - OTHER), range(CHUNKS - OTHER, CHUNKS)
+    main_part, main_cols = pl.ds(0, META + len(main) * width), pl.ds(0, len(main) * width)
+    other_part = pl.ds(META + len(main) * width, OTHER * width)
+    ring_order = list(main[:1]) + [q for pair in zip(other, main[1:]) for q in pair] + list(main[1 + OTHER :])
+    back_order = list(other) + list(main)
+
+    def own(q):
+        return pl.ds((q - len(main)) * width, width)
 
     barrier = pltpu.get_barrier_semaphore()
     with scope("entry"):
@@ -98,7 +108,8 @@
             signal(barrier, at_y(v, 1))
             signal(barrier, at_y(v, 0))
         for v in xs:
-            signal(barrier, at_x(v, c))
+            signal(barrier, at_x(v, 0))
+            signal(barrier, at_x(v, 1))
 
         @pl.when(lead)
         def _():
@@ -140,13 +151,14 @@
         @pl.when(lead)
         def _():
             t1[y * 2 + 1] = tsend[...]
+            a1[x * 2 + 1] = tsend[:, other_part]
 
         @pl.when(jnp.logical_not(lead))
         def _():
             ftok[0] = tsend[...]
 
     with scope("bar"):
-        count = 1 + 2 * (ny - 1) + nx - 1 + 2 * c + (z // hz) * (2 - c)
+        count = 1 + 2 * (ny - 1) + 2 * (nx - 1) + 2 * c + (z // hz) * (2 - c)
         pl.semaphore_wait(barrier, count)
 
         @pl.when(jnp.logical_not(early))
@@ -154,7 +166,15 @@
             signal(ready, across(0))
 
     with scope("ypush"):
-        for q in range(CHUNKS):
+        for q in other:
+            for v in xs:
+                push(tsend.at[:, part(q)], a1.at[x * 2 + c, :, own(q)], so.at[0], r1.at[q], at_x(v))
+
+            @pl.when(jnp.logical_not(lead))
+            def _():
+                push(tsend.at[:, part(q)], a1.at[x * 2 + c, :, own(q)], s0, r1.at[q], partner)
+
+        for q in main:
             for v in ys:
                 push(tsend.at[:, part(q)], t1.at[y * 2 + c, :, part(q)], s1, r1.at[q], at_y(v, 1))
 
@@ -240,6 +260,9 @@
         w = wdn[:, :, :, :, cols(q)].reshape(2 * units, width)
         return jnp.dot(hidden, w, preferred_element_type=F32)
 
+    def arrival(k):
+        return k % 4
+
     def slot(direction, step):
         return direction * steps + step - 1
 
@@ -265,20 +288,18 @@
                 push(ft2.at[x], ft2.at[x], fs.at[2], fr.at[2], at_x(v, 0))
         with scope("s_wait"):
             weights_here()
-            await_bytes(xbuf.at[0:near], rx)
-        with scope("s_gateup"):
-            for q in range(CHUNKS):
-                gate_up(0, near, q)
-        with scope("s_act"):
-            hidden = activations(0, near)
-        with scope("s_down"):
-            for q in range(CHUNKS):
-                v = project(hidden, q)
-                pnear[:, :, :, cols(q)] = v.reshape(near, 2, rows, width).astype(BF16)
-            for s in range(steps - 1, 0, -1):
-                for b in (going_down(s), going_up(s)):
-                    push(pnear.at[b], pnear.at[b], sp, rp.at[s], partner)
-            push(pnear.at[0], pnear.at[0], sp, rp.at[0], partner)
+        for batch, (start, blocks) in enumerate(((0, near - 2), (near - 2, 2))):
+            with scope(f"s_wait{batch}"):
+                await_bytes(xbuf.at[start : start + blocks], rx.at[batch])
+            with scope(f"s_comp{batch}"):
+                for q in range(CHUNKS):
+                    gate_up(start, blocks, q)
+                hidden = activations(start, blocks)
+                for q in range(CHUNKS):
+                    v = project(hidden, q).astype(BF16).reshape(blocks, 2, rows, width)
+                    pnear[start : start + blocks, :, :, cols(q)] = v
+        for b in range(near - 1, -1, -1):
+            push(pnear.at[b], pnear.at[b], sp, rp.at[(b + 1) // 2], partner)
         with scope("f_pack"):
             await_bytes(ft2.at[0 : nx - 1], fr.at[2])
             pickers = [picker(ft2, col, 0) for col in range(2)]
@@ -321,46 +342,60 @@
             for core in range(2):
                 push(fzs.at[core], fin, fs.at[5], fr.at[5], across(core))
 
+    def hop(s, q):
+        for direction, b, later, device in (
+            (0, going_up(s), going_up(s + 1), up),
+            (1, going_down(s), going_down(s + 1), down),
+        ):
+            block = xbuf.at[b, :, :, part(q)]
+            await_bytes(block, ra.at[arrival(s), direction, q])
+            if s < steps:
+                push(block, xbuf.at[later, :, :, part(q)], sa, ra.at[arrival(s + 1), direction, q], device)
+                push(block, block, sx, rx.at[1 if s == steps - 1 else 0], partner)
+
     @pl.when(lead)
     def _():
         with scope("xstage"):
-            for q in range(CHUNKS):
-                await_bytes(t1.at[pl.ds(0, 2 * ny - 1), :, part(q)], r1.at[q])
+            for q in other:
+                await_bytes(a1.at[0 : 2 * nx - 1, :, own(q)], r1.at[q])
+                for v in ys:
+                    push(a1.at[:, :, own(q)], b1.at[y, :, :, own(q)], so.at[1], r2.at[q], at_y(v, 1))
+                b1[y, :, :, own(q)] = a1[:, :, own(q)]
+            for q in main:
+                await_bytes(t1.at[0 : 2 * ny - 1, :, part(q)], r1.at[q])
                 for v in range(ny):
                     for col in range(2):
                         t2[x, col, 2 * v : 2 * v + 2, part(q)] = t1[2 * v + col, :, part(q)]
                 for v in xs:
-                    own = t2.at[x, :, :, part(q)]
-                    push(own, own, s2, r2.at[q], at_x(v))
+                    block = t2.at[x, :, :, part(q)]
+                    push(block, block, s2, r2.at[q], at_x(v))
 
         with scope("pack"):
             pickers = None
-            for q in range(CHUNKS):
-                await_bytes(t2.at[pl.ds(0, nx - 1), :, :, part(q)], r2.at[q])
+            for q in ring_order:
+                if q in main:
+                    await_bytes(t2.at[0 : nx - 1, :, :, part(q)], r2.at[q])
+                else:
+                    await_bytes(b1.at[0 : ny - 1, :, :, own(q)], r2.at[q])
+                    for v in range(ny):
+                        for j in range(2 * nx):
+                            t2[j // 2, j % 2, 2 * v : 2 * v + 2, part(q)] = b1[v, j, :, own(q)]
                 if q == 0:
                     pickers = [picker(t2, col, 0) for col in range(2)]
                 for col in range(2):
                     field = t2[:, col, :, part(q)].reshape(cells, lens[q])
                     picked = jnp.dot(pickers[col], field, preferred_element_type=F32)
                     xbuf[0, col, :, part(q)] = picked.astype(BF16)
-                own = xbuf.at[0, :, :, part(q)]
-                push(own, xbuf.at[going_up(1), :, :, part(q)], sa, ra.at[slot(0, 1), q], up)
-                push(own, xbuf.at[going_down(1), :, :, part(q)], sa, ra.at[slot(1, 1), q], down)
-                push(own, own, sx, rx, partner)
+                block = xbuf.at[0, :, :, part(q)]
+                push(block, xbuf.at[going_up(1), :, :, part(q)], sa, ra.at[arrival(1), 0, q], up)
+                push(block, xbuf.at[going_down(1), :, :, part(q)], sa, ra.at[arrival(1), 1, q], down)
+                push(block, block, sx, rx.at[0], partner)
             weights_here()
 
         with scope("ring"):
             for s in range(1, steps + 1):
-                for q in range(CHUNKS):
-                    for direction, b, later, device in (
-                        (0, going_up(s), going_up(s + 1), up),
-                        (1, going_down(s), going_down(s + 1), down),
-                    ):
-                        block = xbuf.at[b, :, :, part(q)]
-                        await_bytes(block, ra.at[slot(direction, s), q])
-                        if s < steps:
-                            push(block, xbuf.at[later, :, :, part(q)], sa, ra.at[slot(direction, s + 1), q], device)
-                            push(block, block, sx, rx, partner)
+                for q in ring_order:
+                    hop(s, q)
                     if s == steps:
                         gate_up(near, 2, q)
         with scope("act"):
@@ -369,13 +404,13 @@
         def onward(direction, s, q, value, device):
             i = slot(direction, s)
             if s > 1:
-                await_bytes(rrecv.at[i - 1, :, :, cols(q)], rs.at[i - 1, q])
+                await_bytes(rrecv.at[i - 1, :, :, cols(q)], ra.at[arrival(steps + s - 1), direction, q])
                 value = value + rrecv[i - 1, :, :, cols(q)]
             rsend[i, :, :, cols(q)] = value
-            push(rsend.at[i, :, :, cols(q)], rrecv.at[i, :, :, cols(q)], ss, rs.at[i, q], device)
+            push(rsend.at[i, :, :, cols(q)], rrecv.at[i, :, :, cols(q)], ss, ra.at[arrival(steps + s), direction, q], device)
 
         with scope("rs1"):
-            for q in range(CHUNKS):
+            for q in back_order:
                 v = project(hidden, q).astype(BF16).reshape(2, 2, rows, width)
                 onward(0, 1, q, v[1], up)
                 onward(1, 1, q, v[0], down)
@@ -384,26 +419,34 @@
             for s in range(2, steps + 1):
                 at = steps + 1 - s
                 await_bytes(pnear.at[0:2], rp.at[at])
-                for q in range(CHUNKS):
+                for q in back_order:
                     onward(0, s, q, pnear[going_down(at), :, :, cols(q)], up)
                     onward(1, s, q, pnear[going_up(at), :, :, cols(q)], down)
 
         with scope("retx"):
             await_bytes(pnear.at[0], rp.at[0])
-            for q in range(CHUNKS):
+            for q in back_order:
                 one, two = slot(0, steps), slot(1, steps)
-                await_bytes(rrecv.at[two, :, :, cols(q)], rs.at[two, q])
-                await_bytes(rrecv.at[one, :, :, cols(q)], rs.at[one, q])
+                await_bytes(rrecv.at[two, :, :, cols(q)], ra.at[arrival(2 * steps), 1, q])
+                await_bytes(rrecv.at[one, :, :, cols(q)], ra.at[arrival(2 * steps), 0, q])
                 total = pnear[0, :, :, cols(q)].astype(F32) + rrecv[one, :, :, cols(q)].astype(F32)
                 total = (total + rrecv[two, :, :, cols(q)].astype(F32)).astype(BF16)
                 for col in range(2):
-                    placed = jnp.dot(pickers[col], total[col], preferred_element_type=F32)
-                    ysend[:, col, :, cols(q)] = placed.astype(BF16).reshape(nx, 2 * ny, width)
-                for v in xs:
-                    push(ysend.at[v, :, :, cols(q)], yrecv.at[x, :, :, cols(q)], s3, r3.at[q], at_x(v))
+                    placed = jnp.dot(pickers[col], total[col], preferred_element_type=F32).astype(BF16)
+                    if q in main:
+                        ysend[:, col, :, cols(q)] = placed.reshape(nx, 2 * ny, width)
+                    else:
+                        for i in range(nx * ny):
+                            c1[i % ny, 2 * (i // ny) + col, :, own(q)] = placed[2 * i : 2 * i + 2, :]
+                if q in main:
+                    for v in xs:
+                        push(ysend.at[v, :, :, cols(q)], yrecv.at[x, :, :, cols(q)], s3, r3.at[q], at_x(v))
+                else:
+                    for v in ys:
+                        push(c1.at[v, :, :, own(q)], c2.at[y, :, :, own(q)], so.at[2], r3.at[q], at_y(v, 1))
         with scope("rety"):
-            for q in range(CHUNKS):
-                await_bytes(yrecv.at[pl.ds(0, nx - 1), :, :, cols(q)], r3.at[q])
+            for q in main:
+                await_bytes(yrecv.at[0 : nx - 1, :, :, cols(q)], r3.at[q])
                 total = ysend[x, :, :, cols(q)].astype(F32)
                 for v in xs:
                     total += yrecv[v, :, :, cols(q)].astype(F32)
@@ -416,28 +459,41 @@
                         push(fsend.at[v, col, :, cols(q)], frecv.at[y, :, cols(q)], s4, r4.at[q], at_y(v, col))
                 push(fsend.at[y, 0, :, cols(q)], frecv.at[y, :, cols(q)], s0, r4.at[q], partner)
                 frecv[y, :, cols(q)] = fsend[y, 1, :, cols(q)]
+            for q in other:
+                await_bytes(c2.at[0 : ny - 1, :, :, own(q)], r3.at[q])
+                total = c1[y, :, :, own(q)].astype(F32)
+                for v in ys:
+                    total += c2[v, :, :, own(q)].astype(F32)
+                e1[:, :, own(q)] = total.astype(BF16)
+                for v in xs:
+                    for col in range(2):
+                        push(e1.at[2 * v + col, :, own(q)], e2.at[x, :, own(q)], so.at[3], r4.at[q], at_x(v, col))
+                push(e1.at[2 * x, :, own(q)], e2.at[x, :, own(q)], so.at[4], r4.at[q], partner)
+                e2[x, :, own(q)] = e1[2 * x + 1, :, own(q)]
 
     with scope("final"):
+        await_bytes(fin, fr.at[5])
         for q in range(CHUNKS):
+            parts, mine, count = (frecv, cols(q), ny) if q in main else (e2, own(q), nx)
+
             @pl.when(lead)
             def _():
-                await_bytes(frecv.at[0 : ny - 1, :, cols(q)], r4.at[q])
+                await_bytes(parts.at[0 : count - 1, :, mine], r4.at[q])
 
             @pl.when(jnp.logical_not(lead))
             def _():
-                await_bytes(frecv.at[:, :, cols(q)], r4.at[q])
-
-            if q == 0:
-                await_bytes(fin, fr.at[5])
+                await_bytes(parts.at[:, :, mine], r4.at[q])
+
             total = fin[:, cols(q)].astype(F32)
-            for v in range(ny):
-                total += frecv[v, :, cols(q)].astype(F32)
+            for v in range(count):
+                total += parts[v, :, mine].astype(F32)
             total = total.astype(BF16)
             out_ref[0:1, cols(q)] = total[0:1, :]
             out_ref[0:1, pl.ds(half + q * width, width)] = total[1:2, :]
 
     with scope("drain"):
-        await_bytes(t1.at[0 : ny - 1], s1)
+        await_bytes(t1.at[0 : ny - 1, :, main_part], s1)
+        await_bytes(a1.at[0 : nx - 1], so.at[0])
         await_bytes(wgu.at[:, :, 1], ws_sem.at[0])
         await_bytes(wdn.at[:, 1], ws_sem.at[1])
 
@@ -454,13 +510,17 @@
 
         @pl.when(lead)
         def _():
-            await_bytes(t2.at[0 : nx - 1], s2)
+            await_bytes(t2.at[0 : nx - 1, :, :, main_part], s2)
+            await_bytes(b1.at[0 : ny - 1], so.at[1])
+            await_bytes(c2.at[0 : ny - 1], so.at[2])
+            await_bytes(e1.at[0 : 2 * (nx - 1)], so.at[3])
+            await_bytes(e1.at[0], so.at[4])
             await_bytes(xbuf.at[0 : 2 * steps], sa)
             await_bytes(xbuf.at[0:near], sx)
             await_bytes(rsend, ss)
-            await_bytes(yrecv.at[0 : nx - 1], s3)
-            await_bytes(fsend.at[0 : ny - 1], s4)
-            await_bytes(frecv.at[0], s0)
+            await_bytes(yrecv.at[0 : nx - 1, :, :, main_cols], s3)
+            await_bytes(fsend.at[0 : ny - 1, :, :, main_cols], s4)
+            await_bytes(frecv.at[0, :, main_cols], s0)
             await_bytes(tsend, fs.at[0])
 
 
@@ -478,6 +538,7 @@
         exp_node, ffl = w_gate.shape[0], w_gate.shape[1]
         units = 2 * exp_node * ffl
         rows = 2 * CAP
+        lanes = OTHER * (half // CHUNKS)
         sem = pltpu.SemaphoreType.DMA
         one = sem(())
         any_space = pl.BlockSpec(memory_space=pl.ANY)
@@ -515,11 +576,17 @@
                 pltpu.VMEM((ny, 2, 2, half), BF16),
                 pltpu.VMEM((2, 2, half), BF16),
                 pltpu.VMEM((2, half), BF16),
+                pltpu.VMEM((2 * nx, 2, lanes), BF16),
+                pltpu.VMEM((ny, 2 * nx, 2, lanes), BF16),
+                pltpu.VMEM((ny, 2 * nx, 2, lanes), BF16),
+                pltpu.VMEM((ny, 2 * nx, 2, lanes), BF16),
+                pltpu.VMEM((2 * nx, 2, lanes), BF16),
+                pltpu.VMEM((nx, 2, lanes), BF16),
                 sem((3,)), sem((2,)), sem((2,)), sem((2,)),
                 one, one, sem((CHUNKS,)), one, sem((CHUNKS,)),
-                one, sem((2 * steps, CHUNKS)), one, one, one, sem((steps,)),
-                one, sem((2 * steps, CHUNKS)), one, sem((CHUNKS,)), one, sem((CHUNKS,)),
-                sem((6,)), sem((7,)), pltpu.SemaphoreType.REGULAR,
+                one, sem((4, 2, CHUNKS)), one, sem((2,)), one, sem((steps,)),
+                one, one, sem((CHUNKS,)), one, sem((CHUNKS,)),
+                sem((6,)), sem((7,)), pltpu.SemaphoreType.REGULAR, sem((5,)),
             ],
             compiler_params=pltpu.CompilerParams(
                 collective_id=0, has_side_effects=True, vmem_limit_bytes=60 * 1024 * 1024

time: 89 us -> 86.9 us (0.976)
  Pallas kernels: 87.4 us -> 85.2 us
    pallas_call x1, Pallas kernels: 87.4 us -> 85.2 us  [on_device(): pl.pallas_call(functools.partial(layer_kernel, nx, ny, nz), out_shape=jax...]
where the time goes in v4:
time: 86.9 us; the launch traced here: 86.6 us
  Pallas kernels  85.2 us (98%)
  local copies, waits for them, and re-layouts  1.39 us (2%)
    pallas_call x1, Pallas kernels, on_device(): pl.pallas_call(functools.partial(layer_kernel, nx, ny, nz), out_shape=jax...  85.2 us

profile of v4, /device:TPU:1, one launch (start us, length us, event | category | flops | bytes accessed | tf_op | source)
XLA Modules:
  0.0 86.6 jit_solution(2406867111076837207)
XLA Ops:
  0.0 85.2 %layer.1 = bf16[1,7168]{1,0:T(2,128)(2,1)} custom-call(bf16[1,7168]{1,0:T(2,128)(2,1)} %tok_ref.1, bf16[2,32,7168]{2,1,0:T(8,128)(2,1)} %wg_ref.1, bf16[2,32,7168]{2,1,0:T(8,128)(2,1)} %wu_ref.1, bf16[2,32,7168]{2,1,0:T(8,128)(2,1)} %wd_ref.1, s32[1,8]{1,0:T(1,128)} %ids_ref.1, s32[1,8]{1,0:T(1,128)} %gates_ref.1), custom_call_target="tpu_custom_call" | custom-call | tf_op jit(solution)/shard_map/layer/pallas_call | solution.py:546
  85.3 1.4 %copy.8 = bf16[1,7168]{1,0:T(2,128)(2,1)} copy(bf16[1,7168]{1,0:T(2,128)(2,1)} %layer.1) | data formatting | bytes 28672

commit v5 on v4

--- a/solution.py
+++ b/solution.py
@@ -30,7 +30,7 @@
     tokv, idsv, gatesv, tsend, t1, t2, xbuf, wgu, wdn, zbuf, hbuf, pnear, rsend, rrecv,
     ysend, yrecv, fsend, frecv, ftok, ft1, ft2, fxs, fxr, fys, fyr, fzs, fin, a1, b1, c1, c2, e1, e2,
     in_sem, wl_sem, ws_sem, wr_sem, s0, s1, r1, s2, r2, sa, ra, sx, rx, sp, rp, ss, s3, r3, s4, r4,
-    fs, fr, ready, so,
+    fs, fr, ready, so, outv, out_sem,
 ):
     half = wgu.shape[-1]
     width = half // CHUNKS
@@ -56,8 +56,8 @@
     up = (n, lax.rem(z + 1, nz) * 2 + 1)
     down = (n, lax.rem(z + nz - 1, nz) * 2 + 1)
     partner = (n, z * 2 + 1 - c)
-    xs = [lax.rem(x + d, nx) for d in range(1, nx)]
-    ys = [lax.rem(y + d, ny) for d in range(1, ny)]
+    xs = [lax.rem(x + d, nx) for d in sorted(range(1, nx), key=lambda d: -min(d, nx - d))]
+    ys = [lax.rem(y + d, ny) for d in sorted(range(1, ny), key=lambda d: -min(d, ny - d))]
 
     steps = hz - 1
     near = 2 * steps - 1
@@ -488,8 +488,11 @@
             for v in range(count):
                 total += parts[v, :, mine].astype(F32)
             total = total.astype(BF16)
-            out_ref[0:1, cols(q)] = total[0:1, :]
-            out_ref[0:1, pl.ds(half + q * width, width)] = total[1:2, :]
+            outv[0:1, cols(q)] = total[0:1, :]
+            outv[0:1, pl.ds(half + q * width, width)] = total[1:2, :]
+
+    result = pltpu.make_async_copy(outv, out_ref, out_sem)
+    result.start()
 
     with scope("drain"):
         await_bytes(t1.at[0 : ny - 1, :, main_part], s1)
@@ -522,6 +525,8 @@
             await_bytes(fsend.at[0 : ny - 1, :, :, main_cols], s4)
             await_bytes(frecv.at[0, :, main_cols], s0)
             await_bytes(tsend, fs.at[0])
+
+        result.wait()
 
 
 def solution(mesh):
@@ -547,7 +552,7 @@
             functools.partial(layer_kernel, nx, ny, nz),
             out_shape=jax.ShapeDtypeStruct((1, model_width), BF16),
             in_specs=[any_space] * 6,
-            out_specs=vmem,
+            out_specs=any_space,
             scratch_shapes=[
                 pltpu.VMEM((1, model_width), BF16),
                 pltpu.SMEM(expert_ids.shape, jnp.int32),
@@ -587,12 +592,13 @@
                 one, sem((4, 2, CHUNKS)), one, sem((2,)), one, sem((steps,)),
                 one, one, sem((CHUNKS,)), one, sem((CHUNKS,)),
                 sem((6,)), sem((7,)), pltpu.SemaphoreType.REGULAR, sem((5,)),
+                pltpu.VMEM((1, model_width), BF16), one,
             ],
             compiler_params=pltpu.CompilerParams(
-                collective_id=0, has_side_effects=True, vmem_limit_bytes=60 * 1024 * 1024
+                collective_id=0, has_side_effects=True, vmem_limit_bytes=44 * 1024 * 1024
             ),
             name="layer",
-        )(tokens, w_gate, w_up, w_down, expert_ids, gate_ints)
+        )(*(pltpu.with_memory_space_constraint(a, pltpu.HBM) for a in (tokens, w_gate, w_up, w_down, expert_ids, gate_ints)))
 
     both = P(("node", "local"), None)
     weights = P("node", "local", None)

time: 86.9 us -> 84.4 us (0.971)
  Pallas kernels: 85.2 us -> 83.7 us
    pallas_call x1, Pallas kernels: 85.2 us -> 83.7 us  [on_device(): pl.pallas_call(functools.partial(layer_kernel, nx, ny, nz), out_shape=jax...]
where the time goes in v5:
time: 84.4 us; the launch traced here: 84.3 us
  Pallas kernels  83.7 us (99%)
    pallas_call x1, Pallas kernels, on_device(): pl.pallas_call(functools.partial(layer_kernel, nx, ny, nz), out_shape=jax...  83.7 us

profile of v5, /device:TPU:1, one launch (start us, length us, event | category | flops | bytes accessed | tf_op | source)
XLA Modules:
  0.0 84.3 jit_solution(9191774826305647405)
XLA Ops:
  0.0 83.7 %layer.1 = bf16[1,7168]{1,0:T(2,128)(2,1)S(1)} custom-call(bf16[1,7168]{1,0:T(2,128)(2,1)} %tok_ref.1, bf16[2,32,7168]{2,1,0:T(8,128)(2,1)} %wg_ref.1, bf16[2,32,7168]{2,1,0:T(8,128)(2,1)} %wu_ref.1, bf16[2,32,7168]{2,1,0:T(8,128)(2,1)} %wd_ref.1, s32[1,8]{1,0:T(1,128)} %ids_ref.1, s32[1,8]{1,0:T(1,128)} %gates_ref.1), custom_call_target="tpu_custom_call" | custom-call | tf_op jit(solution)/shard_map/layer/pallas_call | solution.py:551
  83.7 0.6 copy.8

commit v6 on v5

--- a/solution.py
+++ b/solution.py
@@ -9,7 +9,8 @@
 
 CAP = 8
 NX = 4
-CHUNKS = 7
+PARTS = (4, 4, 4, 4, 4, 4, 4)
+CHUNKS = len(PARTS)
 OTHER = 2
 META = 128
 BF16 = jnp.bfloat16
@@ -29,14 +30,14 @@
     out_ref,
     tokv, idsv, gatesv, tsend, t1, t2, xbuf, wgu, wdn, zbuf, hbuf, pnear, rsend, rrecv,
     ysend, yrecv, fsend, frecv, ftok, ft1, ft2, fxs, fxr, fys, fyr, fzs, fin, a1, b1, c1, c2, e1, e2,
-    in_sem, wl_sem, ws_sem, wr_sem, s0, s1, r1, s2, r2, sa, ra, sx, rx, sp, rp, ss, s3, r3, s4, r4,
+    in_sem, wl_sem, ws_sem, wr_sem, s0, s1, r1, s2, r2, sa, ra, sx, rx, sp, rp, ss, s3, s4, r4,
     fs, fr, ready, so, outv, out_sem,
 ):
     half = wgu.shape[-1]
-    width = half // CHUNKS
-    offs = [0] + [META + q * width for q in range(1, CHUNKS)]
-    lens = [META + width] + [width] * (CHUNKS - 1)
-    d_off = [META + q * width for q in range(CHUNKS)]
+    widths = [half * part // sum(PARTS) for part in PARTS]
+    starts = [sum(widths[:q]) for q in range(CHUNKS + 1)]
+    offs = [0] + [META + start for start in starts[1:]]
+    lens = [META + widths[0]] + widths[1:]
     hz = nz // 2
     rows = CAP * 2
     ffl = wdn.shape[3]
@@ -90,16 +91,17 @@
         return pl.ds(offs[q], lens[q])
 
     def cols(q):
-        return pl.ds(q * width, width)
+        return pl.ds(starts[q], widths[q])
 
     main, other = range(CHUNKS - OTHER), range(CHUNKS - OTHER, CHUNKS)
-    main_part, main_cols = pl.ds(0, META + len(main) * width), pl.ds(0, len(main) * width)
-    other_part = pl.ds(META + len(main) * width, OTHER * width)
+    split = starts[len(main)]
+    main_part, main_cols = pl.ds(0, META + split), pl.ds(0, split)
+    other_part = pl.ds(META + split, half - split)
     ring_order = list(main[:1]) + [q for pair in zip(other, main[1:]) for q in pair] + list(main[1 + OTHER :])
-    back_order = list(other) + list(main)
+    back_order = [*main[:2], other[0], main[2], other[1], *main[3:]]
 
     def own(q):
-        return pl.ds((q - len(main)) * width, width)
+        return pl.ds(starts[q] - split, widths[q])
 
     barrier = pltpu.get_barrier_semaphore()
     with scope("entry"):
@@ -227,9 +229,9 @@
 
     def gate_up(start, blocks, q):
         count = blocks * 2 * rows
-        piece = xbuf[start : start + blocks, :, :, pl.ds(d_off[q], width)].reshape(count, width)
+        piece = xbuf[start : start + blocks, :, :, pl.ds(META + starts[q], widths[q])].reshape(count, widths[q])
         for h in range(2):
-            w = wgu[h, :, :, :, :, cols(q)].reshape(2 * units, width)
+            w = wgu[h, :, :, :, :, cols(q)].reshape(2 * units, widths[q])
             v = lax.dot_general(piece, w, NT, preferred_element_type=F32)
             for k in range(2):
                 if q == 0:
@@ -257,11 +259,11 @@
         return jnp.concatenate([hbuf[0, 0:count], hbuf[1, 0:count]], axis=1).astype(BF16)
 
     def project(hidden, q):
-        w = wdn[:, :, :, :, cols(q)].reshape(2 * units, width)
+        w = wdn[:, :, :, :, cols(q)].reshape(2 * units, widths[q])
         return jnp.dot(hidden, w, preferred_element_type=F32)
 
     def arrival(k):
-        return k % 4
+        return k % 3
 
     def slot(direction, step):
         return direction * steps + step - 1
@@ -296,7 +298,7 @@
                     gate_up(start, blocks, q)
                 hidden = activations(start, blocks)
                 for q in range(CHUNKS):
-                    v = project(hidden, q).astype(BF16).reshape(blocks, 2, rows, width)
+                    v = project(hidden, q).astype(BF16).reshape(blocks, 2, rows, widths[q])
                     pnear[start : start + blocks, :, :, cols(q)] = v
         for b in range(near - 1, -1, -1):
             push(pnear.at[b], pnear.at[b], sp, rp.at[(b + 1) // 2], partner)
@@ -314,10 +316,10 @@
         with scope("f_retx"):
             pickers = [picker(ft2, col, 1) for col in range(2)]
             for q in range(CHUNKS):
-                v = project(hidden, q).astype(BF16).reshape(2, rows, width)
+                v = project(hidden, q).astype(BF16).reshape(2, rows, widths[q])
                 for col in range(2):
                     placed = jnp.dot(pickers[col], v[col], preferred_element_type=F32)
-                    fxs[:, col, :, cols(q)] = placed.astype(BF16).reshape(nx, 2 * ny, width)
+                    fxs[:, col, :, cols(q)] = placed.astype(BF16).reshape(nx, 2 * ny, widths[q])
             for v in xs:
                 push(fxs.at[v], fxr.at[x], fs.at[3], fr.at[3], at_x(v, 0))
         with scope("f_rety"):
@@ -411,7 +413,7 @@
 
         with scope("rs1"):
             for q in back_order:
-                v = project(hidden, q).astype(BF16).reshape(2, 2, rows, width)
+                v = project(hidden, q).astype(BF16).reshape(2, 2, rows, widths[q])
                 onward(0, 1, q, v[1], up)
                 onward(1, 1, q, v[0], down)
         with scope("rs"):
@@ -434,19 +436,19 @@
                 for col in range(2):
                     placed = jnp.dot(pickers[col], total[col], preferred_element_type=F32).astype(BF16)
                     if q in main:
-                        ysend[:, col, :, cols(q)] = placed.reshape(nx, 2 * ny, width)
+                        ysend[:, col, :, cols(q)] = placed.reshape(nx, 2 * ny, widths[q])
                     else:
                         for i in range(nx * ny):
                             c1[i % ny, 2 * (i // ny) + col, :, own(q)] = placed[2 * i : 2 * i + 2, :]
                 if q in main:
                     for v in xs:
-                        push(ysend.at[v, :, :, cols(q)], yrecv.at[x, :, :, cols(q)], s3, r3.at[q], at_x(v))
+                        push(ysend.at[v, :, :, cols(q)], yrecv.at[x, :, :, cols(q)], s3, r1.at[q], at_x(v))
                 else:
                     for v in ys:
-                        push(c1.at[v, :, :, own(q)], c2.at[y, :, :, own(q)], so.at[2], r3.at[q], at_y(v, 1))
+                        push(c1.at[v, :, :, own(q)], c2.at[y, :, :, own(q)], so.at[2], r1.at[q], at_y(v, 1))
         with scope("rety"):
             for q in main:
-                await_bytes(yrecv.at[0 : nx - 1, :, :, cols(q)], r3.at[q])
+                await_bytes(yrecv.at[0 : nx - 1, :, :, cols(q)], r1.at[q])
                 total = ysend[x, :, :, cols(q)].astype(F32)
                 for v in xs:
                     total += yrecv[v, :, :, cols(q)].astype(F32)
@@ -460,7 +462,7 @@
                 push(fsend.at[y, 0, :, cols(q)], frecv.at[y, :, cols(q)], s0, r4.at[q], partner)
                 frecv[y, :, cols(q)] = fsend[y, 1, :, cols(q)]
             for q in other:
-                await_bytes(c2.at[0 : ny - 1, :, :, own(q)], r3.at[q])
+                await_bytes(c2.at[0 : ny - 1, :, :, own(q)], r1.at[q])
                 total = c1[y, :, :, own(q)].astype(F32)
                 for v in ys:
                     total += c2[v, :, :, own(q)].astype(F32)
@@ -489,7 +491,7 @@
                 total += parts[v, :, mine].astype(F32)
             total = total.astype(BF16)
             outv[0:1, cols(q)] = total[0:1, :]
-            outv[0:1, pl.ds(half + q * width, width)] = total[1:2, :]
+            outv[0:1, pl.ds(half + starts[q], widths[q])] = total[1:2, :]
 
     result = pltpu.make_async_copy(outv, out_ref, out_sem)
     result.start()
@@ -543,7 +545,7 @@
         exp_node, ffl = w_gate.shape[0], w_gate.shape[1]
         units = 2 * exp_node * ffl
         rows = 2 * CAP
-        lanes = OTHER * (half // CHUNKS)
+        lanes = half * sum(PARTS[-OTHER:]) // sum(PARTS)
         sem = pltpu.SemaphoreType.DMA
         one = sem(())
         any_space = pl.BlockSpec(memory_space=pl.ANY)
@@ -589,8 +591,8 @@
                 pltpu.VMEM((nx, 2, lanes), BF16),
                 sem((3,)), sem((2,)), sem((2,)), sem((2,)),
                 one, one, sem((CHUNKS,)), one, sem((CHUNKS,)),
-                one, sem((4, 2, CHUNKS)), one, sem((2,)), one, sem((steps,)),
-                one, one, sem((CHUNKS,)), one, sem((CHUNKS,)),
+                one, sem((3, 2, CHUNKS)), one, sem((2,)), one, sem((steps,)),
+                one, one, one, sem((CHUNKS,)),
                 sem((6,)), sem((7,)), pltpu.SemaphoreType.REGULAR, sem((5,)),
                 pltpu.VMEM((1, model_width), BF16), one,
             ],

time: 84.4 us -> 83.8 us (level)
  no operation moved by 1% of the time
where the time goes in v6:
time: 83.8 us; the launch traced here: 83.6 us
  Pallas kernels  83 us (99%)
    pallas_call x1, Pallas kernels, on_device(): pl.pallas_call(functools.partial(layer_kernel, nx, ny, nz), out_shape=jax...  83 us

profile of v6, /device:TPU:1, one launch (start us, length us, event | category | flops | bytes accessed | tf_op | source)
XLA Modules:
  0.0 83.6 jit_solution(18071579382239177813)
XLA Ops:
  0.0 83.0 %layer.1 = bf16[1,7168]{1,0:T(2,128)(2,1)S(1)} custom-call(bf16[1,7168]{1,0:T(2,128)(2,1)} %tok_ref.1, bf16[2,32,7168]{2,1,0:T(8,128)(2,1)} %wg_ref.1, bf16[2,32,7168]{2,1,0:T(8,128)(2,1)} %wu_ref.1, bf16[2,32,7168]{2,1,0:T(8,128)(2,1)} %wd_ref.1, s32[1,8]{1,0:T(1,128)} %ids_ref.1, s32[1,8]{1,0:T(1,128)} %gates_ref.1), custom_call_target="tpu_custom_call" | custom-call | tf_op jit(solution)/shard_map/layer/pallas_call | solution.py:553
  83.0 0.6 copy.8

commit v7 on v6

--- a/solution.py
+++ b/solution.py
@@ -29,9 +29,9 @@
     tok_ref, wg_ref, wu_ref, wd_ref, ids_ref, gates_ref,
     out_ref,
     tokv, idsv, gatesv, tsend, t1, t2, xbuf, wgu, wdn, zbuf, hbuf, pnear, rsend, rrecv,
-    ysend, yrecv, fsend, frecv, ftok, ft1, ft2, fxs, fxr, fys, fyr, fzs, fin, a1, b1, c1, c2, e1, e2,
+    ysend, yrecv, fsend, frecv, ftok, ft1, ft2, fxs, fxr, fys, fyr, fzs, fin, a1, b1, c1, c2, e1, e2, gbuf,
     in_sem, wl_sem, ws_sem, wr_sem, s0, s1, r1, s2, r2, sa, ra, sx, rx, sp, rp, ss, s3, s4, r4,
-    fs, fr, ready, so, outv, out_sem,
+    fs, fr, ready, so, outv, out_sem, gs, gr, gx,
 ):
     half = wgu.shape[-1]
     widths = [half * part // sum(PARTS) for part in PARTS]
@@ -92,6 +92,9 @@
 
     def cols(q):
         return pl.ds(starts[q], widths[q])
+
+    def data(q):
+        return pl.ds(META + starts[q], widths[q])
 
     main, other = range(CHUNKS - OTHER), range(CHUNKS - OTHER, CHUNKS)
     split = starts[len(main)]
@@ -219,7 +222,12 @@
             shape = (cells, rows)
         r = lax.broadcasted_iota(jnp.int32, shape, side)
         i = lax.broadcasted_iota(jnp.int32, shape, 1 - side)
-        return ones((hit > 0) & (rank == (r // 2).astype(F32)) & (r % 2 == i % 2))
+        picks = ones((hit > 0) & (rank == (r // 2).astype(F32)) & (r % 2 == i % 2))
+        if side == 1:
+            return picks
+        own_row = (r // CAP == col) & (rank == (r % CAP).astype(F32))
+        gates = jnp.dot(ones((hit > 0) & own_row & (i % 2 == 0)), meta, preferred_element_type=F32)
+        return picks, gates
 
     def weights_here():
         await_bytes(wgu.at[:, :, 0], wl_sem.at[0])
@@ -229,7 +237,7 @@
 
     def gate_up(start, blocks, q):
         count = blocks * 2 * rows
-        piece = xbuf[start : start + blocks, :, :, pl.ds(META + starts[q], widths[q])].reshape(count, widths[q])
+        piece = xbuf[start : start + blocks, :, :, cols(q)].reshape(count, widths[q])
         for h in range(2):
             w = wgu[h, :, :, :, :, cols(q)].reshape(2 * units, widths[q])
             v = lax.dot_general(piece, w, NT, preferred_element_type=F32)
@@ -244,12 +252,11 @@
         lane = lax.broadcasted_iota(jnp.int32, (META, units), 0)
         unit = lax.broadcasted_iota(jnp.int32, (META, units), 1)
         chosen = ones(lane == 2 * n + (unit // ffl) % 2)
-        gate_rows = xbuf[start : start + blocks, :, :, 0:META].reshape(count, META)
-        hbuf[0, 0:count] = jnp.dot(gate_rows, chosen, preferred_element_type=F32)
+        gate_rows = gbuf[start : start + blocks].reshape(count // 2, META)
+        scale = jnp.dot(gate_rows, chosen, preferred_element_type=F32) / 8.0
         even, odd = pl.ds(0, count // 2, 2), pl.ds(1, count // 2, 2)
         gate_act = zbuf[0, 0, even, :] + zbuf[1, 0, odd, :]
         up_act = zbuf[0, 1, even, :] + zbuf[1, 1, odd, :]
-        scale = hbuf[0, even, :] / 8.0
         hidden = gate_act / (1.0 + jnp.exp(-gate_act)) * up_act * scale
         none = jnp.zeros_like(hidden)
         hbuf[0, even, :] = hidden
@@ -293,6 +300,7 @@
         for batch, (start, blocks) in enumerate(((0, near - 2), (near - 2, 2))):
             with scope(f"s_wait{batch}"):
                 await_bytes(xbuf.at[start : start + blocks], rx.at[batch])
+                await_bytes(gbuf.at[start : start + blocks], gx.at[batch])
             with scope(f"s_comp{batch}"):
                 for q in range(CHUNKS):
                     gate_up(start, blocks, q)
@@ -304,12 +312,13 @@
             push(pnear.at[b], pnear.at[b], sp, rp.at[(b + 1) // 2], partner)
         with scope("f_pack"):
             await_bytes(ft2.at[0 : nx - 1], fr.at[2])
-            pickers = [picker(ft2, col, 0) for col in range(2)]
+            picked = [picker(ft2, col, 0) for col in range(2)]
+            gbuf[opposite] = (picked[0][1] + picked[1][1]).astype(BF16)
             for col in range(2):
                 for q in range(CHUNKS):
-                    field = ft2[:, col, :, part(q)].reshape(cells, lens[q])
-                    picked = jnp.dot(pickers[col], field, preferred_element_type=F32)
-                    xbuf[opposite, col, :, part(q)] = picked.astype(BF16)
+                    field = ft2[:, col, :, data(q)].reshape(cells, widths[q])
+                    rows_q = jnp.dot(picked[col][0], field, preferred_element_type=F32)
+                    xbuf[opposite, col, :, cols(q)] = rows_q.astype(BF16)
             for q in range(CHUNKS):
                 gate_up(opposite, 1, q)
             hidden = activations(opposite, 1)
@@ -349,11 +358,17 @@
             (0, going_up(s), going_up(s + 1), up),
             (1, going_down(s), going_down(s + 1), down),
         ):
-            block = xbuf.at[b, :, :, part(q)]
+            batch = 1 if s == steps - 1 else 0
+            if q == ring_order[0]:
+                await_bytes(gbuf.at[b], gr.at[arrival(s), direction])
+                if s < steps:
+                    push(gbuf.at[b], gbuf.at[later], gs.at[0], gr.at[arrival(s + 1), direction], device)
+                    push(gbuf.at[b], gbuf.at[b], gs.at[1], gx.at[batch], partner)
+            block = xbuf.at[b, :, :, cols(q)]
             await_bytes(block, ra.at[arrival(s), direction, q])
             if s < steps:
-                push(block, xbuf.at[later, :, :, part(q)], sa, ra.at[arrival(s + 1), direction, q], device)
-                push(block, block, sx, rx.at[1 if s == steps - 1 else 0], partner)
+                push(block, xbuf.at[later, :, :, cols(q)], sa, ra.at[arrival(s + 1), direction, q], device)
+                push(block, block, sx, rx.at[batch], partner)
 
     @pl.when(lead)
     def _():
@@ -383,14 +398,19 @@
                         for j in range(2 * nx):
                             t2[j // 2, j % 2, 2 * v : 2 * v + 2, part(q)] = b1[v, j, :, own(q)]
                 if q == 0:
-                    pickers = [picker(t2, col, 0) for col in range(2)]
+                    picked = [picker(t2, col, 0) for col in range(2)]
+                    pickers = [p for p, _ in picked]
+                    gbuf[0] = (picked[0][1] + picked[1][1]).astype(BF16)
+                    push(gbuf.at[0], gbuf.at[going_up(1)], gs.at[0], gr.at[arrival(1), 0], up)
+                    push(gbuf.at[0], gbuf.at[going_down(1)], gs.at[0], gr.at[arrival(1), 1], down)
+                    push(gbuf.at[0], gbuf.at[0], gs.at[1], gx.at[0], partner)
                 for col in range(2):
-                    field = t2[:, col, :, part(q)].reshape(cells, lens[q])
-                    picked = jnp.dot(pickers[col], field, preferred_element_type=F32)
-                    xbuf[0, col, :, part(q)] = picked.astype(BF16)
-                block = xbuf.at[0, :, :, part(q)]
-                push(block, xbuf.at[going_up(1), :, :, part(q)], sa, ra.at[arrival(1), 0, q], up)
-                push(block, xbuf.at[going_down(1), :, :, part(q)], sa, ra.at[arrival(1), 1, q], down)
+                    field = t2[:, col, :, data(q)].reshape(cells, widths[q])
+                    rows_q = jnp.dot(pickers[col], field, preferred_element_type=F32)
+                    xbuf[0, col, :, cols(q)] = rows_q.astype(BF16)
+                block = xbuf.at[0, :, :, cols(q)]
+                push(block, xbuf.at[going_up(1), :, :, cols(q)], sa, ra.at[arrival(1), 0, q], up)
+                push(block, xbuf.at[going_down(1), :, :, cols(q)], sa, ra.at[arrival(1), 1, q], down)
                 push(block, block, sx, rx.at[0], partner)
             weights_here()
 
@@ -441,8 +461,11 @@
                         for i in range(nx * ny):
                             c1[i % ny, 2 * (i // ny) + col, :, own(q)] = placed[2 * i : 2 * i + 2, :]
                 if q in main:
-                    for v in xs:
-                        push(ysend.at[v, :, :, cols(q)], yrecv.at[x, :, :, cols(q)], s3, r1.at[q], at_x(v))
+                    for turn in range(2):
+                        for v in xs:
+                            @pl.when(v == 0 if turn == 0 else v > 0)
+                            def _():
+                                push(ysend.at[v, :, :, cols(q)], yrecv.at[x, :, :, cols(q)], s3, r1.at[q], at_x(v))
                 else:
                     for v in ys:
                         push(c1.at[v, :, :, own(q)], c2.at[y, :, :, own(q)], so.at[2], r1.at[q], at_y(v, 1))
@@ -456,9 +479,12 @@
                 for v in range(ny):
                     for col in range(2):
                         fsend[v, col, :, cols(q)] = total[col, 2 * v : 2 * v + 2, :]
-                for v in ys:
-                    for col in range(2):
-                        push(fsend.at[v, col, :, cols(q)], frecv.at[y, :, cols(q)], s4, r4.at[q], at_y(v, col))
+                for turn in range(2):
+                    for v in ys:
+                        @pl.when(v == 0 if turn == 0 else v > 0)
+                        def _():
+                            for col in (1, 0):
+                                push(fsend.at[v, col, :, cols(q)], frecv.at[y, :, cols(q)], s4, r4.at[q], at_y(v, col))
                 push(fsend.at[y, 0, :, cols(q)], frecv.at[y, :, cols(q)], s0, r4.at[q], partner)
                 frecv[y, :, cols(q)] = fsend[y, 1, :, cols(q)]
             for q in other:
@@ -522,6 +548,8 @@
             await_bytes(e1.at[0], so.at[4])
             await_bytes(xbuf.at[0 : 2 * steps], sa)
             await_bytes(xbuf.at[0:near], sx)
+            await_bytes(gbuf.at[0 : 2 * steps], gs.at[0])
+            await_bytes(gbuf.at[0:near], gs.at[1])
             await_bytes(rsend, ss)
             await_bytes(yrecv.at[0 : nx - 1, :, :, main_cols], s3)
             await_bytes(fsend.at[0 : ny - 1, :, :, main_cols], s4)
@@ -562,7 +590,7 @@
                 pltpu.VMEM((2, META + half), BF16),
                 pltpu.VMEM((2 * ny, 2, META + half), BF16),
                 pltpu.VMEM((nx, 2, 2 * ny, META + half), BF16),
-                pltpu.VMEM((nz, 2, rows, META + half), BF16),
+                pltpu.VMEM((nz, 2, rows, half), BF16),
                 pltpu.VMEM((2, 2, 2, exp_node, ffl, half), BF16),
                 pltpu.VMEM((2, 2, exp_node, ffl, half), BF16),
                 pltpu.VMEM((2, 2, near * 2 * rows, units), F32),
@@ -589,12 +617,14 @@
                 pltpu.VMEM((ny, 2 * nx, 2, lanes), BF16),
                 pltpu.VMEM((2 * nx, 2, lanes), BF16),
                 pltpu.VMEM((nx, 2, lanes), BF16),
+                pltpu.VMEM((nz, rows, META), BF16),
                 sem((3,)), sem((2,)), sem((2,)), sem((2,)),
                 one, one, sem((CHUNKS,)), one, sem((CHUNKS,)),
                 one, sem((3, 2, CHUNKS)), one, sem((2,)), one, sem((steps,)),
                 one, one, one, sem((CHUNKS,)),
                 sem((6,)), sem((7,)), pltpu.SemaphoreType.REGULAR, sem((5,)),
                 pltpu.VMEM((1, model_width), BF16), one,
+                sem((2,)), sem((3, 2)), sem((2,)),
             ],
             compiler_params=pltpu.CompilerParams(
                 collective_id=0, has_side_effects=True, vmem_limit_bytes=44 * 1024 * 1024

time: 83.8 us -> 83.6 us (level)
  no operation moved by 1% of the time
where the time goes in v7:
time: 83.6 us; the launch traced here: 83.4 us
  Pallas kernels  82.8 us (99%)
    pallas_call x1, Pallas kernels, on_device(): pl.pallas_call(functools.partial(layer_kernel, nx, ny, nz), out_shape=jax...  82.8 us

profile of v7, /device:TPU:1, one launch (start us, length us, event | category | flops | bytes accessed | tf_op | source)
XLA Modules:
  0.0 83.4 jit_solution(15804942512012984270)
XLA Ops:
  0.0 82.8 %layer.1 = bf16[1,7168]{1,0:T(2,128)(2,1)S(1)} custom-call(bf16[1,7168]{1,0:T(2,128)(2,1)} %tok_ref.1, bf16[2,32,7168]{2,1,0:T(8,128)(2,1)} %wg_ref.1, bf16[2,32,7168]{2,1,0:T(8,128)(2,1)} %wu_ref.1, bf16[2,32,7168]{2,1,0:T(8,128)(2,1)} %wd_ref.1, s32[1,8]{1,0:T(1,128)} %ids_ref.1, s32[1,8]{1,0:T(1,128)} %gates_ref.1), custom_call_target="tpu_custom_call" | custom-call | tf_op jit(solution)/shard_map/layer/pallas_call | solution.py:581
  82.8 0.6 copy.8

commit v8 on v7

--- a/solution.py
+++ b/solution.py
@@ -400,10 +400,6 @@
                 if q == 0:
                     picked = [picker(t2, col, 0) for col in range(2)]
                     pickers = [p for p, _ in picked]
-                    gbuf[0] = (picked[0][1] + picked[1][1]).astype(BF16)
-                    push(gbuf.at[0], gbuf.at[going_up(1)], gs.at[0], gr.at[arrival(1), 0], up)
-                    push(gbuf.at[0], gbuf.at[going_down(1)], gs.at[0], gr.at[arrival(1), 1], down)
-                    push(gbuf.at[0], gbuf.at[0], gs.at[1], gx.at[0], partner)
                 for col in range(2):
                     field = t2[:, col, :, data(q)].reshape(cells, widths[q])
                     rows_q = jnp.dot(pickers[col], field, preferred_element_type=F32)
@@ -412,6 +408,11 @@
                 push(block, xbuf.at[going_up(1), :, :, cols(q)], sa, ra.at[arrival(1), 0, q], up)
                 push(block, xbuf.at[going_down(1), :, :, cols(q)], sa, ra.at[arrival(1), 1, q], down)
                 push(block, block, sx, rx.at[0], partner)
+                if q == 0:
+                    gbuf[0] = (picked[0][1] + picked[1][1]).astype(BF16)
+                    push(gbuf.at[0], gbuf.at[going_up(1)], gs.at[0], gr.at[arrival(1), 0], up)
+                    push(gbuf.at[0], gbuf.at[going_down(1)], gs.at[0], gr.at[arrival(1), 1], down)
+                    push(gbuf.at[0], gbuf.at[0], gs.at[1], gx.at[0], partner)
             weights_here()
 
         with scope("ring"):
@@ -501,7 +502,7 @@
 
     with scope("final"):
         await_bytes(fin, fr.at[5])
-        for q in range(CHUNKS):
+        for q in [*main[:-1], *other, main[-1]]:
             parts, mine, count = (frecv, cols(q), ny) if q in main else (e2, own(q), nx)
 
             @pl.when(lead)

time: 83.6 us -> 83.5 us (level)
  no operation moved by 1% of the time
where the time goes in v8:
time: 83.5 us; the launch traced here: 83.4 us
  Pallas kernels  82.8 us (99%)
    pallas_call x1, Pallas kernels, on_device(): pl.pallas_call(functools.partial(layer_kernel, nx, ny, nz), out_shape=jax...  82.8 us

profile of v8, /device:TPU:1, one launch (start us, length us, event | category | flops | bytes accessed | tf_op | source)
XLA Modules:
  0.0 83.4 jit_solution(12117581336118139735)
XLA Ops:
  0.0 82.8 %layer.1 = bf16[1,7168]{1,0:T(2,128)(2,1)S(1)} custom-call(bf16[1,7168]{1,0:T(2,128)(2,1)} %tok_ref.1, bf16[2,32,7168]{2,1,0:T(8,128)(2,1)} %wg_ref.1, bf16[2,32,7168]{2,1,0:T(8,128)(2,1)} %wu_ref.1, bf16[2,32,7168]{2,1,0:T(8,128)(2,1)} %wd_ref.1, s32[1,8]{1,0:T(1,128)} %ids_ref.1, s32[1,8]{1,0:T(1,128)} %gates_ref.1), custom_call_target="tpu_custom_call" | custom-call | tf_op jit(solution)/shard_map/layer/pallas_call | solution.py:582
  82.8 0.6 copy.8
